TPU v7x, 32 devices: a whole 2x2x4 slice. The times are simulated.
32 devices in a mesh: fsdp: 8 (over y, x, core), dp: 4 (over z).
Axes of the slice: x: 2, y: 2, z: 4, core: 2. Of those that a mesh axis runs over, the one named last changes fastest.
Arguments:
- hidden: bfloat16 [8192, 14336], P(('fsdp', 'dp')), may hold values from -6 to 6
- cotangent: bfloat16 [8192, 4096], P(('fsdp', 'dp')), may hold values from -6 to 6
- tiles: bfloat16 [64, 128, 128], P('fsdp'), may hold values from -0.25 to 0.25
- tile_rows: int32 [64], P('fsdp'), may hold values from 0 to 111, as said below
- tile_cols: int32 [64], P('fsdp'), may hold values from 0 to 31, as said below
- counts: int32 [8], P('fsdp'), may hold values from 1 to 8, as said below
Outputs:
- layer_out: bfloat16 [8192, 4096], P(('fsdp', 'dp'))
- hidden_grad: bfloat16 [8192, 14336], P(('fsdp', 'dp'))
- weight_grad: float32 [64, 128, 128], P('fsdp')
Inputs may be any that keep to these rules, and one draw needn't show every extreme that they name: `tile_rows`: every slot (live or not) names a different block; the row block is below 112. `tile_cols`: the column block is below 32. `counts`: some owner has all 8 slots live in every draw.
All inputs are finite; a program needn't handle non-finite values.
Results may differ from a plain program's by a relative error of at most 0.0085.
Values may be sent and summed in bfloat16 or wider, within the bound.
A program may use at most 192 MiB of HBM per device.

v0:
```python
import functools
import math

import jax
import jax.numpy as jnp
from jax import lax
from jax.experimental import pallas as pl
from jax.experimental.pallas import tpu as pltpu
from jax.sharding import PartitionSpec as P

MESH = pl.DeviceIdType.MESH
F32 = jnp.float32
BF16 = jnp.bfloat16


def exchange_kernel(
    n, dp, root,
    rows_s, cols_s, cnt_s, tiles_hbm, hid_hbm, cot_hbm,
    meta_out, tiles_out, wg_out,
    hid_v, cot_v, tiles_v, meta_v, meta_s, acc, sbuf, rbuf, fin, zs, zr, za, sqz, sqf,
    in_sem, out_sem, meta_ss, meta_rs, ag_ss, ag_rs, rs_ss, rs_rs,
    zs_ss, zs_rs, za_ss, za_rs, qz_ss, qz_rs, qf_ss, qf_rs,
):
    me = lax.axis_index("fsdp")
    z = lax.axis_index("dp")
    maxb, edge = tiles_hbm.shape[0], tiles_hbm.shape[1]
    half = maxb // 2
    per = maxb // dp
    stages = n.bit_length() - 1
    chip_bits = stages - 1
    orders = [list(range(1, stages)), list(range(stages - 1, 0, -1))]
    core = lax.rem(me, 2)

    def bit_of(b):
        return lax.rem(me // (2 ** b), 2)

    def flip(value_me, b):
        return value_me + (1 - 2 * bit_of(b)) * (2 ** b)

    def fetch(source, target, sem):
        def step(i, carry):
            at = pl.ds(pl.multiple_of(i * edge, edge), edge)
            pltpu.make_async_copy(source.at[:, at], target.at[i], sem).start()
            return carry
        lax.fori_loop(0, target.shape[0], step, 0)

    own_copy = pltpu.make_async_copy(tiles_hbm, tiles_v.at[me], in_sem.at[2])
    own_copy.start()
    fetch(cot_hbm, cot_v, in_sem.at[1])
    fetch(hid_hbm, hid_v, in_sem.at[0])

    barrier = pltpu.get_barrier_semaphore()
    for k in range(1, n):
        pl.semaphore_signal(
            barrier, inc=1, device_id={"fsdp": lax.rem(me + k, n)}, device_id_type=MESH
        )
    for k in range(1, dp):
        pl.semaphore_signal(
            barrier, inc=1, device_id={"dp": lax.rem(z + k, dp)}, device_id_type=MESH
        )
    lane = lax.broadcasted_iota(jnp.int32, (8, 128), 1)
    sub = lax.broadcasted_iota(jnp.int32, (8, 128), 0)
    meta = jnp.where(sub == 2, cnt_s[0], 0)
    for j in range(maxb):
        meta = jnp.where((sub == 0) & (lane == j), rows_s[j], meta)
        meta = jnp.where((sub == 1) & (lane == j), cols_s[j], meta)
    meta_v[me] = meta
    own_copy.wait()
    pl.semaphore_wait(barrier, n - 1 + dp - 1)

    meta_copies = []
    for k in range(1, n):
        copy = pltpu.make_async_remote_copy(
            meta_v.at[me], meta_v.at[me], meta_ss.at[k - 1], meta_rs.at[k - 1],
            device_id={"fsdp": lax.rem(me + k, n)}, device_id_type=MESH,
        )
        copy.start()
        meta_copies.append(copy)

    ag_copies = {}

    def ag_send(p, i, e):
        bits = orders[p] + [0]
        owner = me
        for t in range(len(bits)):
            if (e >> t) & 1:
                owner = flip(owner, bits[t])
        piece = tiles_v.at[owner, pl.ds(p * half, half)]
        where = 2 ** i - 1 + e
        copy = pltpu.make_async_remote_copy(
            piece, piece, ag_ss.at[p, where], ag_rs.at[p, where],
            device_id={"fsdp": flip(me, bits[i])}, device_id_type=MESH,
        )
        copy.start()
        ag_copies[p, i, e] = copy

    for i in range(stages):
        for p in range(2):
            ag_send(p, i, 0)

    for copy in meta_copies:
        copy.wait_recv()
    to_smem = pltpu.make_async_copy(meta_v, meta_s, in_sem.at[3])
    to_smem.start()
    to_smem.wait()
    meta_back = pltpu.make_async_copy(meta_v, meta_out, out_sem.at[0])
    meta_back.start()
    pltpu.make_async_copy(cot_v, cot_v, in_sem.at[1]).wait()
    pltpu.make_async_copy(hid_v, hid_v, in_sem.at[0]).wait()

    def owner_at(p, e, core_bit):
        owner = core_bit
        for t, b in enumerate(orders[p]):
            ebit = lax.rem(e // (2 ** (chip_bits - 1 - t)), 2)
            owner = owner + lax.rem(bit_of(b) + 1 + ebit, 2) * (2 ** b)
        return owner

    def term(owner, j):
        return lax.dot_general(
            hid_v[meta_s[owner, 0, j]], cot_v[meta_s[owner, 1, j]],
            (((0,), (0,)), ((), ())), preferred_element_type=F32,
        )

    chips = n // 2
    offsets = [0]
    for t in range(stages):
        offsets.append(offsets[-1] + (n >> (t + 1)))

    def rs_copy(p, t, e):
        where = offsets[t] + e
        bit = 0 if t == 0 else orders[p][t - 1]
        return pltpu.make_async_remote_copy(
            sbuf.at[p, where], rbuf.at[p, where], rs_ss.at[p, where], rs_rs.at[p, where],
            device_id={"fsdp": flip(me, bit)}, device_id_type=MESH,
        )

    def foreign(e, carry):
        for p in range(2):
            owner = owner_at(p, e, 1 - core)
            for j in range(half):
                sbuf[p, e, j] = term(owner, p * half + j).astype(BF16)
            rs_copy(p, 0, e).start()
        return carry

    lax.fori_loop(0, chips, foreign, 0)

    for i in range(chip_bits):
        for p in range(2):
            for e in range(2 ** i):
                ag_copies[p, i, e].wait_recv()
                for i2 in range(i + 1, stages):
                    ag_send(p, i2, e + 2 ** i)

    def own(e, carry):
        for p in range(2):
            owner = owner_at(p, e, core)
            for j in range(half):
                acc[p, e, j] = term(owner, p * half + j)
        return carry

    lax.fori_loop(0, chips, own, 0)

    start = 0
    for t in range(stages):
        m = n >> (t + 1)
        sent = m // 2
        for e in range(m):
            for p in range(2):
                rs_copy(p, t, e).wait_recv()
                total = acc[p, start + e] + rbuf[p, offsets[t] + e].astype(F32)
                if e < sent:
                    sbuf[p, offsets[t + 1] + e] = total.astype(BF16)
                    rs_copy(p, t + 1, e).start()
                elif m > 1:
                    acc[p, start + e] = total
                else:
                    fin[pl.ds(p * half, half)] = total
                    for q in range(half // per):
                        zs[p * (half // per) + q] = total[q * per:(q + 1) * per].astype(BF16)
        start += sent

    def z_peer(r):
        return lax.rem(z + r, dp)

    z_copies = []
    for r in range(1, dp):
        copy = pltpu.make_async_remote_copy(
            zs.at[z_peer(r)], zr.at[r - 1], zs_ss.at[r - 1], zs_rs.at[r - 1],
            device_id={"dp": z_peer(r)}, device_id_type=MESH,
        )
        copy.start()
        z_copies.append(copy)

    for p in range(2):
        for e in range(2 ** chip_bits):
            ag_copies[p, chip_bits, e].wait_recv()
    tiles_back = pltpu.make_async_copy(tiles_v, tiles_out, out_sem.at[1])
    tiles_back.start()

    piece = fin[pl.ds(z * per, per)]
    for r in range(1, dp):
        z_copies[r - 1].wait_recv()
        piece = piece + zr[r - 1].astype(F32)
    slot = z * per + lax.broadcasted_iota(jnp.int32, piece.shape, 0)
    piece = piece * jnp.clip(cnt_s[0] - slot, 0, 1).astype(F32)
    za[z] = piece.astype(BF16)
    sqz[z] = jnp.sum((piece * piece).reshape(-1, 8, 128), axis=0)
    a_copies, q_copies = [], []
    for r in range(1, dp):
        copy = pltpu.make_async_remote_copy(
            sqz.at[z], sqz.at[z], qz_ss.at[r - 1], qz_rs.at[r - 1],
            device_id={"dp": z_peer(r)}, device_id_type=MESH,
        )
        copy.start()
        q_copies.append(copy)
    for r in range(1, dp):
        copy = pltpu.make_async_remote_copy(
            za.at[z], za.at[z], za_ss.at[r - 1], za_rs.at[r - 1],
            device_id={"dp": z_peer(r)}, device_id_type=MESH,
        )
        copy.start()
        a_copies.append(copy)
    for copy in q_copies:
        copy.wait_recv()
    sqf[me] = jnp.sum(sqz[...], axis=0)
    f_copies = []
    for k in range(1, n):
        copy = pltpu.make_async_remote_copy(
            sqf.at[me], sqf.at[me], qf_ss.at[k - 1], qf_rs.at[k - 1],
            device_id={"fsdp": lax.rem(me + k, n)}, device_id_type=MESH,
        )
        copy.start()
        f_copies.append(copy)
    entries = meta_s[0, 2, 0]
    for k in range(1, n):
        entries = entries + meta_s[k, 2, 0]
    for copy in a_copies + f_copies:
        copy.wait_recv()
    squares = jnp.sum(jnp.sum(sqf[...], axis=0), axis=(0, 1), keepdims=True)
    live = jnp.full((1, 1), entries, jnp.int32).astype(F32) * edge * edge
    spread = jnp.sqrt(squares / live)
    factor = jnp.minimum(1.0, 0.5 * root / spread) / root
    for q in range(dp):
        for i in range(per):
            wg_out[q * per + i] = za[q, i].astype(F32) * factor

    for copy in meta_copies + list(ag_copies.values()) + z_copies + q_copies + a_copies + f_copies:
        copy.wait_send()
    for t in range(stages):
        for e in range(n >> (t + 1)):
            for p in range(2):
                rs_copy(p, t, e).wait_send()
    meta_back.wait()
    tiles_back.wait()


def project_kernel(
    n, maxb,
    meta_s, tiles_hbm, hid_hbm, cot_hbm,
    layer_hbm, grad_hbm,
    tiles_v, cot_v, hid_v, gacc, gout, lacc, lout, zero_v, values,
    row_left, row_seen, col_left, col_seen,
    in_sem, hid_sem, g_sem, l_sem,
):
    edge = zero_v.shape[1]
    tile_copy = pltpu.make_async_copy(tiles_hbm, tiles_v, in_sem.at[0])
    cot_copy = pltpu.make_async_copy(cot_hbm, cot_v, in_sem.at[1])
    tile_copy.start()
    cot_copy.start()
    zero_v[...] = jnp.zeros_like(zero_v)

    def clear(left, seen):
        def step(i, carry):
            left[i] = 0
            seen[i] = 0
            return carry
        lax.fori_loop(0, left.shape[0], step, 0)

    clear(row_left, row_seen)
    clear(col_left, col_seen)

    def columns(i):
        return pl.ds(pl.multiple_of(i * edge, edge), edge)

    def each_live(visit):
        def owner(o, carry):
            def slot(j, inner):
                visit(o, j, meta_s[o, 0, j], meta_s[o, 1, j])
                return inner
            return lax.fori_loop(0, meta_s[o, 2, 0], slot, carry)
        lax.fori_loop(0, n, owner, 0)

    def fetch(o, j, row, col):
        pltpu.make_async_copy(hid_hbm.at[:, columns(row)], hid_v.at[o, j], hid_sem).start()
        row_left[row] = row_left[row] + 1
        col_left[col] = col_left[col] + 1

    each_live(fetch)

    def blank(left, target, sem):
        def step(i, carry):
            @pl.when(left[i] == 0)
            def _():
                pltpu.make_async_copy(zero_v, target.at[:, columns(i)], sem).start()
            return carry
        lax.fori_loop(0, left.shape[0], step, 0)

    blank(row_left, grad_hbm, g_sem)
    blank(col_left, layer_hbm, l_sem)
    tile_copy.wait()
    cot_copy.wait()

    def add_block(at, value, left, seen, total, out, target, sem):
        remaining = left[at] - 1
        first = seen[at] == 0
        left[at] = remaining
        seen[at] = 1

        @pl.when(first & (remaining == 0))
        def _():
            out[at] = value[...].astype(BF16)

        @pl.when(first & (remaining > 0))
        def _():
            total[at] = value[...]

        @pl.when(jnp.logical_not(first))
        def _():
            summed = total[at] + value[...]
            total[at] = summed
            out[at] = summed.astype(BF16)

        @pl.when(remaining == 0)
        def _():
            pltpu.make_async_copy(out.at[at], target.at[:, columns(at)], sem).start()

    def backward(o, carry):
        for j in range(maxb):
            values[j] = lax.dot_general(
                cot_v[:, columns(meta_s[o, 1, j])], tiles_v[o, j], (((1,), (1,)), ((), ())),
                preferred_element_type=F32,
            )

        def slot(j, inner):
            add_block(
                meta_s[o, 0, j], values.at[j], row_left, row_seen, gacc, gout, grad_hbm, g_sem
            )
            return inner

        return lax.fori_loop(0, meta_s[o, 2, 0], slot, carry)

    lax.fori_loop(0, n, backward, 0)

    def arrived(o, j, row, col):
        pltpu.make_async_copy(hid_hbm.at[:, columns(row)], hid_v.at[o, j], hid_sem).wait()

    each_live(arrived)

    def forward(o, carry):
        for j in range(maxb):
            values[j] = jnp.dot(hid_v[o, j], tiles_v[o, j], preferred_element_type=F32)

        def slot(j, inner):
            add_block(
                meta_s[o, 1, j], values.at[j], col_left, col_seen, lacc, lout, layer_hbm, l_sem
            )
            return inner

        return lax.fori_loop(0, meta_s[o, 2, 0], slot, carry)

    lax.fori_loop(0, n, forward, 0)
    pltpu.make_async_copy(grad_hbm, grad_hbm, g_sem).wait()
    pltpu.make_async_copy(layer_hbm, layer_hbm, l_sem).wait()


def shards(n, dp, hidden, cotangent, tiles, tile_rows, tile_cols, counts):
    tokens, width_ff = hidden.shape
    width_model = cotangent.shape[1]
    maxb, edge, _ = tiles.shape
    blocks_ff, blocks_model = width_ff // edge, width_model // edge
    root = math.sqrt(tokens * n * dp)
    half, per = maxb // 2, maxb // dp
    hbm = pl.BlockSpec(memory_space=pl.ANY)
    smem = pl.BlockSpec(memory_space=pltpu.SMEM)
    vmem = pl.BlockSpec(memory_space=pltpu.VMEM)
    dma = pltpu.SemaphoreType.DMA
    meta, gathered, weight_grad = pl.pallas_call(
        functools.partial(exchange_kernel, n, dp, root),
        out_shape=(
            jax.ShapeDtypeStruct((n, 8, 128), jnp.int32),
            jax.ShapeDtypeStruct((n, maxb, edge, edge), BF16),
            jax.ShapeDtypeStruct((maxb, edge, edge), F32),
        ),
        in_specs=[smem, smem, smem, hbm, hbm, hbm],
        out_specs=(hbm, hbm, vmem),
        scratch_shapes=[
            pltpu.VMEM((blocks_ff, tokens, edge), BF16),
            pltpu.VMEM((blocks_model, tokens, edge), BF16),
            pltpu.VMEM((n, maxb, edge, edge), BF16),
            pltpu.VMEM((n, 8, 128), jnp.int32),
            pltpu.SMEM((n, 8, 128), jnp.int32),
            pltpu.VMEM((2, n // 2, half, edge, edge), F32),
            pltpu.VMEM((2, n - 1, half, edge, edge), BF16),
            pltpu.VMEM((2, n - 1, half, edge, edge), BF16),
            pltpu.VMEM((maxb, edge, edge), F32),
            pltpu.VMEM((dp, per, edge, edge), BF16),
            pltpu.VMEM((dp - 1, per, edge, edge), BF16),
            pltpu.VMEM((dp, per, edge, edge), BF16),
            pltpu.VMEM((dp, 8, 128), F32),
            pltpu.VMEM((n, 8, 128), F32),
            dma((4,)), dma((2,)),
            dma((n - 1,)), dma((n - 1,)),
            dma((2, n - 1)), dma((2, n - 1)),
            dma((2, n - 1)), dma((2, n - 1)),
            dma((dp - 1,)), dma((dp - 1,)),
            dma((dp - 1,)), dma((dp - 1,)),
            dma((dp - 1,)), dma((dp - 1,)),
            dma((n - 1,)), dma((n - 1,)),
        ],
        compiler_params=pltpu.CompilerParams(
            collective_id=0, has_side_effects=True, vmem_limit_bytes=60 * 2 ** 20
        ),
        name="exchange",
    )(tile_rows, tile_cols, counts, tiles, hidden, cotangent)

    layer_out, hidden_grad = pl.pallas_call(
        functools.partial(project_kernel, n, maxb),
        out_shape=(
            jax.ShapeDtypeStruct(cotangent.shape, BF16),
            jax.ShapeDtypeStruct(hidden.shape, BF16),
        ),
        in_specs=[smem, hbm, hbm, hbm],
        out_specs=(hbm, hbm),
        scratch_shapes=[
            pltpu.VMEM((n, maxb, edge, edge), BF16),
            pltpu.VMEM(cotangent.shape, BF16),
            pltpu.VMEM((n, maxb, tokens, edge), BF16),
            pltpu.VMEM((blocks_ff, tokens, edge), F32),
            pltpu.VMEM((blocks_ff, tokens, edge), BF16),
            pltpu.VMEM((blocks_model, tokens, edge), F32),
            pltpu.VMEM((blocks_model, tokens, edge), BF16),
            pltpu.VMEM((tokens, edge), BF16),
            pltpu.VMEM((maxb, tokens, edge), F32),
            pltpu.SMEM((blocks_ff,), jnp.int32),
            pltpu.SMEM((blocks_ff,), jnp.int32),
            pltpu.SMEM((blocks_model,), jnp.int32),
            pltpu.SMEM((blocks_model,), jnp.int32),
            dma((2,)), dma, dma, dma,
        ],
        compiler_params=pltpu.CompilerParams(vmem_limit_bytes=62 * 2 ** 20),
        name="project",
    )(meta, gathered, hidden, cotangent)
    return layer_out, hidden_grad, weight_grad


def solution(mesh):
    placed = (
        P(("fsdp", "dp"), None),
        P(("fsdp", "dp"), None),
        P("fsdp", None, None),
        P("fsdp"),
        P("fsdp"),
        P("fsdp"),
    )
    return jax.shard_map(
        functools.partial(shards, mesh.shape["fsdp"], mesh.shape["dp"]),
        mesh=mesh,
        in_specs=placed,
        out_specs=(P(("fsdp", "dp"), None), P(("fsdp", "dp"), None), P("fsdp", None, None)),
        check_vma=False,
    )
```

profile of v0, /device:TPU:0, one launch (start us, length us, event | category | flops | bytes accessed | tf_op | source)
XLA Modules:
  0.0 61.2 jit_solution(6509944032430782735)
XLA Ops:
  1.3 46.2 %exchange.1 = (s32[8,8,128]{2,1,0:T(8,128)}, bf16[8,8,128,128]{3,2,1,0:T(8,128)(2,1)}, f32[8,128,128]{2,1,0:T(8,128)}) custom-call(s32[8]{0:T(128)} %rows_s.1, s32[8]{0:T(128)} %cols_s.1, s32[1]{0:T(128)S(6)} %copy.10.cnt_s, bf16[8,128,128]{2,1,0:T(8,128)(2,1)} %tiles_hbm.1, bf16[256,14336]{1,0:T(8,128)(2,1)} %hid_hbm.3, bf16[256,4096]{1,0:T(8,128)(2,1)} %cot_hbm.3), custom_call_target="tpu_custom_call" | custom-call | tf_op jit(solution)/shard_map/exchange/pallas_call | solution.py:387
  47.5 0.0 copy-start
  47.5 12.9 %project.1 = (bf16[256,4096]{1,0:T(8,128)(2,1)}, bf16[256,14336]{1,0:T(8,128)(2,1)}) custom-call(s32[8,8,128]{2,1,0:T(8,128)} %get-tuple-element.8.meta_s, bf16[8,8,128,128]{3,2,1,0:T(8,128)(2,1)} %get-tuple-element.9.tiles_hbm, bf16[256,14336]{1,0:T(8,128)(2,1)} %hid_hbm.3, bf16[256,4096]{1,0:T(8,128)(2,1)} %cot_hbm.3), custom_call_target="tpu_custom_call" | custom-call | tf_op jit(solution)/shard_map/project/pallas_call | solution.py:426
  60.4 0.0 copy-done
  60.4 0.8 %copy.11 = f32[8,128,128]{2,1,0:T(8,128)} copy(f32[8,128,128]{2,1,0:T(8,128)S(1)} %copy-done) | data formatting | bytes 1048576
Async XLA Ops:
  47.5 12.9 %copy-start = (f32[8,128,128]{2,1,0:T(8,128)S(1)}, f32[8,128,128]{2,1,0:T(8,128)}, u32[]{:S(2)}) copy-start(f32[8,128,128]{2,1,0:T(8,128)} %get-tuple-element.18) | copy-start | bytes 1572868
where the time goes:
time: 61.4 us; the launch traced here: 61.2 us
  Pallas kernels  59.1 us (96%)
  between operations  1.31 us (2%)
  local copies, waits for them, and re-layouts  0.8 us (1%)
    pallas_call x1, Pallas kernels, shards(): pl.pallas_call(functools.partial(exchange_kernel, n, dp, root), out_shape...  46.2 us
    pallas_call x1, Pallas kernels, shards(): pl.pallas_call(functools.partial(project_kernel, n, maxb), out_shape=(jax...  12.9 us

commit v1 on v0

--- a/solution.py
+++ b/solution.py
@@ -373,6 +373,457 @@
     pltpu.make_async_copy(layer_hbm, layer_hbm, l_sem).wait()
 
 
+def fused_kernel(
+    n, dp, root,
+    rows_s, cols_s, cnt_s, tiles_hbm, hid_hbm, cot_hbm,
+    grad_out, layer_out, wg_out, table_out,
+    hid_v, cot_v, tiles_v, meta_v, full_v, full_s, table_s,
+    acc, sbuf, rbuf, fin, zs, zr, za, sqf, grad_q, layer_q,
+    in_sem, meta_ss, meta_rs, ag_ss, ag_rs, rs_ss, rs_rs,
+    zs_ss, zs_rs, za_ss, za_rs, sq_ss, sq_rs,
+):
+    me = lax.axis_index("fsdp")
+    z = lax.axis_index("dp")
+    maxb, edge = tiles_hbm.shape[0], tiles_hbm.shape[1]
+    slots = n * maxb
+    half = maxb // 2
+    rows_z = 2 * edge // dp
+    stages = n.bit_length() - 1
+    chip_bits = stages - 1
+    chips = n // 2
+    orders = [list(range(1, stages)), list(range(stages - 1, 0, -1))]
+
+    def bit_of(b):
+        return lax.rem(me // (2 ** b), 2)
+
+    def relative(x):
+        other = me
+        for b in range(stages):
+            if (x >> b) & 1:
+                other = other + (1 - 2 * bit_of(b)) * (2 ** b)
+        return other
+
+    def z_peer(r):
+        return lax.rem(z + r, dp)
+
+    def fetch(source, target, sem):
+        def step(i, carry):
+            at = pl.ds(pl.multiple_of(i * edge, edge), edge)
+            pltpu.make_async_copy(source.at[:, at], target.at[i], sem).start()
+            return carry
+        lax.fori_loop(0, target.shape[0], step, 0)
+
+    own_copy = pltpu.make_async_copy(tiles_hbm, tiles_v.at[0], in_sem.at[2])
+    own_copy.start()
+    barrier = pltpu.get_barrier_semaphore()
+    for x in range(1, n):
+        pl.semaphore_signal(
+            barrier, inc=1, device_id={"fsdp": relative(x)}, device_id_type=MESH
+        )
+    for r in range(1, dp):
+        pl.semaphore_signal(
+            barrier, inc=1, device_id={"dp": z_peer(r)}, device_id_type=MESH
+        )
+    fetch(cot_hbm, cot_v, in_sem.at[1])
+    fetch(hid_hbm, hid_v, in_sem.at[0])
+
+    lane = lax.broadcasted_iota(jnp.int32, (8, 128), 1)
+    sub = lax.broadcasted_iota(jnp.int32, (8, 128), 0)
+    meta = jnp.where(sub == 2, cnt_s[0], 0)
+    for j in range(maxb):
+        here = lax.rem(lane, maxb) == j
+        meta = jnp.where((sub == 0) & here, rows_s[j], meta)
+        meta = jnp.where((sub == 1) & here, cols_s[j], meta)
+    meta_v[0] = meta
+    grad_q[slots] = jnp.zeros(grad_q.shape[1:], F32)
+    layer_q[slots] = jnp.zeros(layer_q.shape[1:], F32)
+    grad_out[slots] = jnp.zeros(grad_out.shape[1:], BF16)
+    layer_out[slots] = jnp.zeros(layer_out.shape[1:], BF16)
+    own_copy.wait()
+    pl.semaphore_wait(barrier, n - 1 + dp - 1)
+
+    meta_copies = []
+    for x in range(1, n):
+        copy = pltpu.make_async_remote_copy(
+            meta_v.at[0], meta_v.at[x], meta_ss.at[x - 1], meta_rs.at[x - 1],
+            device_id={"fsdp": relative(x)}, device_id_type=MESH,
+        )
+        copy.start()
+        meta_copies.append(copy)
+
+    ag_copies = {}
+    ag_done = set()
+
+    def ag_send(p, i, e):
+        bits = orders[p] + [0]
+        owner = 0
+        for t in range(len(bits)):
+            if (e >> t) & 1:
+                owner |= 1 << bits[t]
+        where = 2 ** i - 1 + e
+        part = pl.ds(p * half, half)
+        copy = pltpu.make_async_remote_copy(
+            tiles_v.at[owner, part], tiles_v.at[owner | (1 << bits[i]), part],
+            ag_ss.at[p, where], ag_rs.at[p, where],
+            device_id={"fsdp": relative(1 << bits[i])}, device_id_type=MESH,
+        )
+        copy.start()
+        ag_copies[p, i, e] = copy
+
+    def ag_wait(p, i, e):
+        if (p, i, e) not in ag_done:
+            ag_done.add((p, i, e))
+            ag_copies[p, i, e].wait_recv()
+
+    for i in range(stages):
+        for p in range(2):
+            ag_send(p, i, 0)
+
+    for copy in meta_copies:
+        copy.wait_recv()
+    full = jnp.zeros((8, 128), jnp.int32)
+    for x in range(n):
+        full = jnp.where(lane // maxb == x, meta_v[x], full)
+    full_v[...] = full
+    to_smem = pltpu.make_async_copy(full_v, full_s, in_sem.at[3])
+    to_smem.start()
+
+    wide = lax.broadcasted_iota(jnp.int32, (slots, 128), 1)
+    tall = lax.broadcasted_iota(jnp.int32, (slots, 128), 0)
+    alive = lax.rem(lane[0:1], maxb) < full[2:3]
+    table = jnp.full((8, 128), slots, jnp.int32)
+    for k in range(2):
+        named = jnp.broadcast_to(jnp.where(alive, full[k:k + 1], -1), (slots, 128))
+        named_t = jnp.sum(jnp.where(wide == tall, named, 0), axis=1, keepdims=True)
+        before = jnp.max(
+            jnp.where((named_t == named) & (tall < wide), tall, -1), axis=0, keepdims=True
+        )
+        last = jnp.max(jnp.where(named_t == wide, tall, -1), axis=0, keepdims=True)
+        table = jnp.where(sub == k, jnp.where(before < 0, slots, before), table)
+        table = jnp.where(sub == 2 + k, jnp.where(last < 0, slots, last), table)
+    table_out[...] = table
+    table_copy = pltpu.make_async_copy(table_out, table_s, in_sem.at[4])
+    table_copy.start()
+    to_smem.wait()
+    pltpu.make_async_copy(cot_v, cot_v, in_sem.at[1]).wait()
+    pltpu.make_async_copy(hid_v, hid_v, in_sem.at[0]).wait()
+
+    def term(q):
+        return lax.dot_general(
+            hid_v[full_s[0, q]], cot_v[full_s[1, q]],
+            (((0,), (0,)), ((), ())), preferred_element_type=F32,
+        )
+
+    def owner_at(p, e):
+        owner = 0
+        for t, b in enumerate(orders[p]):
+            if not (e >> (chip_bits - 1 - t)) & 1:
+                owner |= 1 << b
+        return owner
+
+    offsets = [0]
+    for t in range(stages):
+        offsets.append(offsets[-1] + (n >> (t + 1)))
+
+    def rs_copy(p, t, e, c):
+        where = offsets[t] + e
+        bit = 0 if t == 0 else orders[p][t - 1]
+        return pltpu.make_async_remote_copy(
+            sbuf.at[p, where, c], rbuf.at[p, where, c],
+            rs_ss.at[p, where, c], rs_rs.at[p, where, c],
+            device_id={"fsdp": relative(1 << bit)}, device_id_type=MESH,
+        )
+
+    def foreign(c):
+        for e in range(chips):
+            for p in range(2):
+                q = (owner_at(p, e) | 1) * maxb + p * half + c
+                sbuf[p, e, c] = term(q).astype(BF16)
+                rs_copy(p, 0, e, c).start()
+
+    def own(c):
+        for e in range(chips):
+            for p in range(2):
+                acc[p, e, c] = term(owner_at(p, e) * maxb + p * half + c)
+
+    starts = [0]
+    for t in range(stages):
+        starts.append(starts[-1] + (n >> (t + 1)) // 2)
+
+    def reduce_step(t, c):
+        m = n >> (t + 1)
+        for e in range(m):
+            for p in range(2):
+                rs_copy(p, t, e, c).wait_recv()
+                total = acc[p, starts[t] + e, c] + rbuf[p, offsets[t] + e, c].astype(F32)
+                if e < m // 2:
+                    sbuf[p, offsets[t + 1] + e, c] = total.astype(BF16)
+                    rs_copy(p, t + 1, e, c).start()
+                elif m > 1:
+                    acc[p, starts[t] + e, c] = total
+                else:
+                    at = pl.ds(p * edge, edge)
+                    fin[c, at] = total
+                    zs[c, at] = total.astype(BF16)
+        if m == 1:
+            for r in range(1, dp):
+                z_copy(c, r).start()
+
+    def z_rows(index):
+        return pl.ds(pl.multiple_of(index * rows_z, rows_z), rows_z)
+
+    def z_copy(c, r):
+        return pltpu.make_async_remote_copy(
+            zs.at[c, z_rows(z_peer(r))], zr.at[c, r - 1], zs_ss.at[c, r - 1], zs_rs.at[c, r - 1],
+            device_id={"dp": z_peer(r)}, device_id_type=MESH,
+        )
+
+    def a_copy(c, r):
+        return pltpu.make_async_remote_copy(
+            za.at[c, z_rows(z)], za.at[c, z_rows(z)], za_ss.at[c, r - 1], za_rs.at[c, r - 1],
+            device_id={"dp": z_peer(r)}, device_id_type=MESH,
+        )
+
+    def z_step(c, squares):
+        piece = fin[c, z_rows(z)]
+        for r in range(1, dp):
+            z_copy(c, r).wait_recv()
+            piece = piece + zr[c, r - 1].astype(F32)
+        row = z * rows_z + lax.broadcasted_iota(jnp.int32, piece.shape, 0)
+        slot = (row // edge) * half + c
+        piece = piece * jnp.clip(cnt_s[0] - slot, 0, 1).astype(F32)
+        za[c, z_rows(z)] = piece.astype(BF16)
+        for r in range(1, dp):
+            a_copy(c, r).start()
+        return squares + jnp.sum((piece * piece).reshape(-1, 8, 128), axis=0)
+
+    def project(x):
+        def load(j):
+            q = x * maxb + j
+            backward = lax.dot_general(
+                cot_v[full_s[1, q]], tiles_v[x, j], (((1,), (1,)), ((), ())),
+                preferred_element_type=F32,
+            )
+            forward = jnp.dot(hid_v[full_s[0, q]], tiles_v[x, j], preferred_element_type=F32)
+            return q, backward, forward
+        for j in range(maxb):
+            q, backward, forward = load(j)
+            backward = backward + grad_q[table_s[0, q]]
+            grad_q[q] = backward
+            grad_out[q] = backward.astype(BF16)
+            forward = forward + layer_q[table_s[1, q]]
+            layer_q[q] = forward
+            layer_out[q] = forward.astype(BF16)
+
+    def arrived(x):
+        for p in range(2):
+            bits = orders[p] + [0]
+            index = [t for t in range(stages) if (x >> bits[t]) & 1]
+            if index:
+                e = sum(1 << t for t in index[:-1])
+                ag_wait(p, index[-1], e)
+
+    foreign(0)
+
+    def first(c, carry):
+        @pl.when(c + 1 < half)
+        def _():
+            foreign(c + 1)
+        own(c)
+        reduce_step(0, c)
+        return carry
+
+    lax.fori_loop(0, half, first, 0)
+
+    for i in range(chip_bits):
+        for p in range(2):
+            ag_wait(p, i, 0)
+            ag_send(p, chip_bits, 2 ** i)
+    table_copy.wait()
+    early = [x for x in range(n) if bin(x >> 1).count("1") < 2]
+    for x in early:
+        arrived(x)
+
+    def second(k, carry):
+        project(k)
+        reduce_step(1, k)
+        return carry
+
+    lax.fori_loop(0, half, second, 0)
+    for i in range(1, chip_bits):
+        for p in range(2):
+            for e in range(1, 2 ** i):
+                ag_wait(p, i - 1, e - 2 ** (i - 1))
+                ag_send(p, i, e)
+
+    def third(k, carry):
+        @pl.when(half + k < len(early))
+        def _():
+            project(half + k)
+        reduce_step(2, k)
+        return carry
+
+    lax.fori_loop(0, half, third, 0)
+
+    for i in range(1, chip_bits):
+        for p in range(2):
+            for e in range(1, 2 ** i):
+                ag_wait(p, i, e)
+                ag_send(p, chip_bits, e + 2 ** i)
+
+    squares = lax.fori_loop(0, half, z_step, jnp.zeros((8, 128), F32))
+    place = me * dp + z
+    sqf[place] = jnp.sum(squares, axis=0, keepdims=True)
+    sq_copies = []
+    for x in range(n):
+        for r in range(dp):
+            if x or r:
+                copy = pltpu.make_async_remote_copy(
+                    sqf.at[place], sqf.at[place], sq_ss, sq_rs,
+                    device_id={"fsdp": relative(x), "dp": z_peer(r)}, device_id_type=MESH,
+                )
+                copy.start()
+                sq_copies.append(copy)
+
+    for x in range(len(early), n):
+        arrived(x)
+
+    def rest(x, carry):
+        project(x)
+        return carry
+
+    lax.fori_loop(len(early), n, rest, 0)
+
+    entries = full_s[2, 0]
+    for x in range(1, n):
+        entries = entries + full_s[2, x * maxb]
+    others = sqf.at[pl.ds(0, n * dp - 1)]
+    pltpu.make_async_copy(others, others, sq_rs).wait()
+    squares = jnp.sum(jnp.sum(sqf[...], axis=0), axis=1, keepdims=True)
+    live = jnp.full((1, 1), entries, jnp.int32).astype(F32) * edge * edge
+    spread = jnp.sqrt(squares / live)
+    factor = jnp.minimum(1.0, 0.5 * root / spread) / root
+
+    def finish(c, carry):
+        for r in range(1, dp):
+            a_copy(c, r).wait_recv()
+        for p in range(2):
+            wg_out[p * half + c] = za[c, pl.ds(p * edge, edge)].astype(F32) * factor
+        return carry
+
+    lax.fori_loop(0, half, finish, 0)
+
+    for copy in meta_copies + list(ag_copies.values()):
+        copy.wait_send()
+    pltpu.make_async_copy(others, others, sq_ss).wait()
+
+    def drain(c, carry):
+        for t in range(stages):
+            for e in range(n >> (t + 1)):
+                for p in range(2):
+                    rs_copy(p, t, e, c).wait_send()
+        for r in range(1, dp):
+            z_copy(c, r).wait_send()
+            a_copy(c, r).wait_send()
+        return carry
+
+    lax.fori_loop(0, half, drain, 0)
+
+
+def write_kernel(
+    grad_v, layer_v, wg_v, table_v,
+    layer_hbm, grad_hbm, wg_hbm,
+    table_s, t_sem, w_sem, g_sem, l_sem,
+):
+    edge = grad_v.shape[2]
+    table_copy = pltpu.make_async_copy(table_v, table_s, t_sem)
+    table_copy.start()
+    wg_copy = pltpu.make_async_copy(wg_v, wg_hbm, w_sem)
+    wg_copy.start()
+    table_copy.wait()
+
+    def write(row, source, target, sem):
+        def step(i, carry):
+            at = pl.ds(pl.multiple_of(i * edge, edge), edge)
+            pltpu.make_async_copy(source.at[table_s[row, i]], target.at[:, at], sem).start()
+            return carry
+        lax.fori_loop(0, target.shape[1] // edge, step, 0)
+
+    write(2, grad_v, grad_hbm, g_sem)
+    write(3, layer_v, layer_hbm, l_sem)
+    pltpu.make_async_copy(grad_hbm, grad_hbm, g_sem).wait()
+    pltpu.make_async_copy(layer_hbm, layer_hbm, l_sem).wait()
+    wg_copy.wait()
+
+
+def fused(n, dp, hidden, cotangent, tiles, tile_rows, tile_cols, counts):
+    tokens, width_ff = hidden.shape
+    width_model = cotangent.shape[1]
+    maxb, edge, _ = tiles.shape
+    blocks_ff, blocks_model = width_ff // edge, width_model // edge
+    root = math.sqrt(tokens * n * dp)
+    slots, half = n * maxb, maxb // 2
+    rows_z = 2 * edge // dp
+    hbm = pl.BlockSpec(memory_space=pltpu.HBM)
+    smem = pl.BlockSpec(memory_space=pltpu.SMEM)
+    vmem = pl.BlockSpec(memory_space=pltpu.VMEM)
+    dma = pltpu.SemaphoreType.DMA
+    grad, layer, weight, table = pl.pallas_call(
+        functools.partial(fused_kernel, n, dp, root),
+        out_shape=(
+            pltpu.VMEM((slots + 1, tokens, edge), BF16),
+            pltpu.VMEM((slots + 1, tokens, edge), BF16),
+            pltpu.VMEM((maxb, edge, edge), F32),
+            pltpu.VMEM((8, 128), jnp.int32),
+        ),
+        in_specs=[smem, smem, smem, hbm, hbm, hbm],
+        out_specs=(vmem, vmem, vmem, vmem),
+        scratch_shapes=[
+            pltpu.VMEM((blocks_ff, tokens, edge), BF16),
+            pltpu.VMEM((blocks_model, tokens, edge), BF16),
+            pltpu.VMEM((n, maxb, edge, edge), BF16),
+            pltpu.VMEM((n, 8, 128), jnp.int32),
+            pltpu.VMEM((8, 128), jnp.int32),
+            pltpu.SMEM((8, 128), jnp.int32),
+            pltpu.SMEM((8, 128), jnp.int32),
+            pltpu.VMEM((2, n // 2, half, edge, edge), F32),
+            pltpu.VMEM((2, n - 1, half, edge, edge), BF16),
+            pltpu.VMEM((2, n - 1, half, edge, edge), BF16),
+            pltpu.VMEM((half, 2 * edge, edge), F32),
+            pltpu.VMEM((half, 2 * edge, edge), BF16),
+            pltpu.VMEM((half, dp - 1, rows_z, edge), BF16),
+            pltpu.VMEM((half, 2 * edge, edge), BF16),
+            pltpu.VMEM((n * dp, 1, 128), F32),
+            pltpu.VMEM((slots + 1, tokens, edge), F32),
+            pltpu.VMEM((slots + 1, tokens, edge), F32),
+            dma((5,)),
+            dma((n - 1,)), dma((n - 1,)),
+            dma((2, n - 1)), dma((2, n - 1)),
+            dma((2, n - 1, half)), dma((2, n - 1, half)),
+            dma((half, dp - 1)), dma((half, dp - 1)),
+            dma((half, dp - 1)), dma((half, dp - 1)),
+            dma, dma,
+        ],
+        compiler_params=pltpu.CompilerParams(
+            collective_id=0, has_side_effects=True, vmem_limit_bytes=44 * 2 ** 20
+        ),
+        name="fused",
+    )(tile_rows, tile_cols, counts, tiles, hidden, cotangent)
+    return pl.pallas_call(
+        write_kernel,
+        out_shape=(
+            jax.ShapeDtypeStruct(cotangent.shape, BF16),
+            jax.ShapeDtypeStruct(hidden.shape, BF16),
+            jax.ShapeDtypeStruct(tiles.shape, F32),
+        ),
+        in_specs=[vmem, vmem, vmem, vmem],
+        out_specs=(hbm, hbm, hbm),
+        scratch_shapes=[pltpu.SMEM((8, 128), jnp.int32), dma, dma, dma, dma],
+        compiler_params=pltpu.CompilerParams(vmem_limit_bytes=16 * 2 ** 20),
+        name="write",
+    )(grad, layer, weight, table)
+
+
 def shards(n, dp, hidden, cotangent, tiles, tile_rows, tile_cols, counts):
     tokens, width_ff = hidden.shape
     width_model = cotangent.shape[1]
@@ -380,6 +831,9 @@
     blocks_ff, blocks_model = width_ff // edge, width_model // edge
     root = math.sqrt(tokens * n * dp)
     half, per = maxb // 2, maxb // dp
+    sums = n * maxb * tokens * edge * 12
+    if n == 8 and dp % 2 == 0 and max(n * maxb, blocks_ff, blocks_model) <= 128 and sums <= 28 * 2 ** 20:
+        return fused(n, dp, hidden, cotangent, tiles, tile_rows, tile_cols, counts)
     hbm = pl.BlockSpec(memory_space=pl.ANY)
     smem = pl.BlockSpec(memory_space=pltpu.SMEM)
     vmem = pl.BlockSpec(memory_space=pltpu.VMEM)

time: 61.4 us -> 48.1 us (0.78)
  Pallas kernels: 59.1 us -> 44.4 us
  local copies, waits for them, and re-layouts: 0.8 us -> 2.25 us
    pallas_call x2, Pallas kernels: 59.1 us -> 44.4 us  [the longest x1 40.3 us: fused(): pl.pallas_call(functools.partial(fused_kernel, n, dp, root), out_shape=(p...]
    unnamed x3 -> x6, local copies, waits for them, and re-layouts: 0.8 us -> 2.25 us
where the time goes in v1:
time: 48.1 us; the launch traced here: 48 us
  Pallas kernels  44.4 us (92%)
  local copies, waits for them, and re-layouts  2.25 us (5%)
  between operations  1.3 us (3%)
    pallas_call x1, Pallas kernels, fused(): pl.pallas_call(functools.partial(fused_kernel, n, dp, root), out_shape=(p...  40.3 us
    pallas_call x1, Pallas kernels, fused(): pl.pallas_call(write_kernel, out_shape=(jax.ShapeDtypeStruct(cotangent.sh...  4.15 us
    unnamed x6, local copies, waits for them, and re-layouts  2.25 us

profile of v1, /device:TPU:0, one launch (start us, length us, event | category | flops | bytes accessed | tf_op | source)
XLA Modules:
  0.0 48.0 jit_solution(1086735999343165287)
XLA Ops:
  1.3 0.0 copy-start
  1.3 0.9 %copy-done = bf16[8,128,128]{2,1,0:T(8,128)(2,1)S(1)} copy-done((bf16[8,128,128]{2,1,0:T(8,128)(2,1)S(1)}, bf16[8,128,128]{2,1,0:T(8,128)(2,1)}, u32[]{:S(2)}) %copy-start) | copy-done | bytes 262168
  2.2 0.0 copy-start.1
  2.2 0.7 %copy-done.1 = s32[8]{0:T(128)S(1)} copy-done((s32[8]{0:T(128)S(1)}, s32[8]{0:T(128)}, u32[]{:S(2)}) %copy-start.1) | copy-done | bytes 56
  2.9 0.0 copy-start.2
  2.9 0.7 %copy-done.2 = s32[8]{0:T(128)S(1)} copy-done((s32[8]{0:T(128)S(1)}, s32[8]{0:T(128)}, u32[]{:S(2)}) %copy-start.2) | copy-done | bytes 56
  3.5 40.3 %fused.1 = (bf16[65,256,128]{2,1,0:T(8,128)(2,1)S(1)}, bf16[65,256,128]{2,1,0:T(8,128)(2,1)S(1)}, f32[8,128,128]{2,1,0:T(8,128)S(1)}, s32[8,128]{1,0:T(8,128)S(1)}) custom-call(s32[8]{0:T(128)S(1)} %copy-done.1, s32[8]{0:T(128)S(1)} %copy-done.2, s32[1]{0:T(128)S(6)} %copy.9.cnt_s, bf16[8,128,128]{2,1,0:T(8,128)(2,1)S(1)} %copy-done, ...), custom_call_target="tpu_custom_call" | custom-call | tf_op jit(solution)/shard_map/fused/pallas_call | solution.py:771
  43.8 4.1 %write.1 = (bf16[256,4096]{1,0:T(8,128)(2,1)}, bf16[256,14336]{1,0:T(8,128)(2,1)}, f32[8,128,128]{2,1,0:T(8,128)}) custom-call(bf16[65,256,128]{2,1,0:T(8,128)(2,1)S(1)} %get-tuple-element.7.grad_v, bf16[65,256,128]{2,1,0:T(8,128)(2,1)S(1)} %get-tuple-element.8.layer_v, f32[8,128,128]{2,1,0:T(8,128)S(1)} %get-tuple-element.9.wg_v, ...), custom_call_target="tpu_custom_call" | custom-call | tf_op jit(solution)/shard_map/write/pallas_call | solution.py:812
Async XLA Ops:
  1.3 1.0 %copy-start = (bf16[8,128,128]{2,1,0:T(8,128)(2,1)S(1)}, bf16[8,128,128]{2,1,0:T(8,128)(2,1)}, u32[]{:S(2)}) copy-start(bf16[8,128,128]{2,1,0:T(8,128)(2,1)} %tiles_hbm.1) | copy-start | bytes 786436
  2.2 0.7 %copy-start.1 = (s32[8]{0:T(128)S(1)}, s32[8]{0:T(128)}, u32[]{:S(2)}) copy-start(s32[8]{0:T(128)} %rows_s.1) | copy-start | bytes 100
  2.9 0.7 %copy-start.2 = (s32[8]{0:T(128)S(1)}, s32[8]{0:T(128)}, u32[]{:S(2)}) copy-start(s32[8]{0:T(128)} %cols_s.1) | copy-start | bytes 100

commit v2 on v1

--- a/solution.py
+++ b/solution.py
@@ -375,9 +375,9 @@
 
 def fused_kernel(
     n, dp, root,
-    rows_s, cols_s, cnt_s, tiles_hbm, hid_hbm, cot_hbm,
+    rows_hbm, cols_hbm, cnt_s, tiles_hbm, hid_hbm, cot_hbm,
     grad_out, layer_out, wg_out, table_out,
-    hid_v, cot_v, tiles_v, meta_v, full_v, full_s, table_s,
+    rows_s, cols_s, hid_v, cot_v, tiles_v, meta_v, full_v, full_s, table_s,
     acc, sbuf, rbuf, fin, zs, zr, za, sqf, grad_q, layer_q,
     in_sem, meta_ss, meta_rs, ag_ss, ag_rs, rs_ss, rs_rs,
     zs_ss, zs_rs, za_ss, za_rs, sq_ss, sq_rs,
@@ -413,6 +413,10 @@
             return carry
         lax.fori_loop(0, target.shape[0], step, 0)
 
+    rows_copy = pltpu.make_async_copy(rows_hbm, rows_s, in_sem.at[5])
+    rows_copy.start()
+    cols_copy = pltpu.make_async_copy(cols_hbm, cols_s, in_sem.at[6])
+    cols_copy.start()
     own_copy = pltpu.make_async_copy(tiles_hbm, tiles_v.at[0], in_sem.at[2])
     own_copy.start()
     barrier = pltpu.get_barrier_semaphore()
@@ -430,6 +434,8 @@
     lane = lax.broadcasted_iota(jnp.int32, (8, 128), 1)
     sub = lax.broadcasted_iota(jnp.int32, (8, 128), 0)
     meta = jnp.where(sub == 2, cnt_s[0], 0)
+    rows_copy.wait()
+    cols_copy.wait()
     for j in range(maxb):
         here = lax.rem(lane, maxb) == j
         meta = jnp.where((sub == 0) & here, rows_s[j], meta)
@@ -763,6 +769,7 @@
     blocks_ff, blocks_model = width_ff // edge, width_model // edge
     root = math.sqrt(tokens * n * dp)
     slots, half = n * maxb, maxb // 2
+    in_hbm = functools.partial(pltpu.with_memory_space_constraint, memory_space=pltpu.HBM)
     rows_z = 2 * edge // dp
     hbm = pl.BlockSpec(memory_space=pltpu.HBM)
     smem = pl.BlockSpec(memory_space=pltpu.SMEM)
@@ -776,9 +783,11 @@
             pltpu.VMEM((maxb, edge, edge), F32),
             pltpu.VMEM((8, 128), jnp.int32),
         ),
-        in_specs=[smem, smem, smem, hbm, hbm, hbm],
+        in_specs=[hbm, hbm, smem, hbm, hbm, hbm],
         out_specs=(vmem, vmem, vmem, vmem),
         scratch_shapes=[
+            pltpu.SMEM(tile_rows.shape, jnp.int32),
+            pltpu.SMEM(tile_cols.shape, jnp.int32),
             pltpu.VMEM((blocks_ff, tokens, edge), BF16),
             pltpu.VMEM((blocks_model, tokens, edge), BF16),
             pltpu.VMEM((n, maxb, edge, edge), BF16),
@@ -796,7 +805,7 @@
             pltpu.VMEM((n * dp, 1, 128), F32),
             pltpu.VMEM((slots + 1, tokens, edge), F32),
             pltpu.VMEM((slots + 1, tokens, edge), F32),
-            dma((5,)),
+            dma((7,)),
             dma((n - 1,)), dma((n - 1,)),
             dma((2, n - 1)), dma((2, n - 1)),
             dma((2, n - 1, half)), dma((2, n - 1, half)),
@@ -808,7 +817,7 @@
             collective_id=0, has_side_effects=True, vmem_limit_bytes=44 * 2 ** 20
         ),
         name="fused",
-    )(tile_rows, tile_cols, counts, tiles, hidden, cotangent)
+    )(in_hbm(tile_rows), in_hbm(tile_cols), counts, in_hbm(tiles), in_hbm(hidden), in_hbm(cotangent))
     return pl.pallas_call(
         write_kernel,
         out_shape=(

time: 48.1 us -> 45.3 us (0.942)
  local copies, waits for them, and re-layouts: 2.25 us -> 0 us
  Pallas kernels: 44.4 us -> 43.9 us
    unnamed x6 -> x0, local copies, waits for them, and re-layouts: 2.25 us -> none
    pallas_call x1, Pallas kernels: 40.3 us -> 39.7 us  [fused(): pl.pallas_call(functools.partial(fused_kernel, n, dp, root), out_shape=(p...]
where the time goes in v2:
time: 45.3 us; the launch traced here: 45.2 us
  Pallas kernels  43.9 us (97%)
  between operations  1.29 us (3%)
    pallas_call x1, Pallas kernels, fused(): pl.pallas_call(functools.partial(fused_kernel, n, dp, root), out_shape=(p...  39.7 us
    pallas_call x1, Pallas kernels, fused(): pl.pallas_call(write_kernel, out_shape=(jax.ShapeDtypeStruct(cotangent.sh...  4.15 us

profile of v2, /device:TPU:0, one launch (start us, length us, event | category | flops | bytes accessed | tf_op | source)
XLA Modules:
  0.0 45.2 jit_solution(230733758209430734)
XLA Ops:
  1.3 39.7 %fused.1 = (bf16[65,256,128]{2,1,0:T(8,128)(2,1)S(1)}, bf16[65,256,128]{2,1,0:T(8,128)(2,1)S(1)}, f32[8,128,128]{2,1,0:T(8,128)S(1)}, s32[8,128]{1,0:T(8,128)S(1)}) custom-call(s32[8]{0:T(128)} %rows_hbm.1, s32[8]{0:T(128)} %cols_hbm.1, s32[1]{0:T(128)S(6)} %copy.9.cnt_s, bf16[8,128,128]{2,1,0:T(8,128)(2,1)} %tiles_hbm.1, bf16[256,14336]{1,0:T(8,128)(2,1)} %hid_hbm.1, ...), custom_call_target="tpu_custom_call" | custom-call | tf_op jit(solution)/shard_map/fused/pallas_call | solution.py:778
  41.0 4.1 %write.1 = (bf16[256,4096]{1,0:T(8,128)(2,1)}, bf16[256,14336]{1,0:T(8,128)(2,1)}, f32[8,128,128]{2,1,0:T(8,128)}) custom-call(bf16[65,256,128]{2,1,0:T(8,128)(2,1)S(1)} %get-tuple-element.7.grad_v, bf16[65,256,128]{2,1,0:T(8,128)(2,1)S(1)} %get-tuple-element.8.layer_v, f32[8,128,128]{2,1,0:T(8,128)S(1)} %get-tuple-element.9.wg_v, ...), custom_call_target="tpu_custom_call" | custom-call | tf_op jit(solution)/shard_map/write/pallas_call | solution.py:821

commit v3 on v2

--- a/solution.py
+++ b/solution.py
@@ -406,6 +406,12 @@
     def z_peer(r):
         return lax.rem(z + r, dp)
 
+    near = [x for x in range(n) if bin(x >> 1).count("1") < 2]
+    far = [x for x in range(n) if x not in near]
+    queue = [0, 1] + [x for x in near if x > 1 and x % 2 == 0]
+    queue += [x for x in near if x > 1 and x % 2 == 1] + far
+    place = [queue.index(x) for x in range(n)]
+
     def fetch(source, target, sem):
         def step(i, carry):
             at = pl.ds(pl.multiple_of(i * edge, edge), edge)
@@ -460,63 +466,52 @@
     ag_copies = {}
     ag_done = set()
 
-    def ag_send(p, i, e):
+    def ag_send(p, i, e, h):
         bits = orders[p] + [0]
         owner = 0
         for t in range(len(bits)):
             if (e >> t) & 1:
                 owner |= 1 << bits[t]
         where = 2 ** i - 1 + e
-        part = pl.ds(p * half, half)
+        part = pl.ds(p * half + h * (half // 2), half // 2)
         copy = pltpu.make_async_remote_copy(
-            tiles_v.at[owner, part], tiles_v.at[owner | (1 << bits[i]), part],
-            ag_ss.at[p, where], ag_rs.at[p, where],
+            tiles_v.at[place[owner], part], tiles_v.at[place[owner | (1 << bits[i])], part],
+            ag_ss.at[p, where, h], ag_rs.at[p, where, h],
             device_id={"fsdp": relative(1 << bits[i])}, device_id_type=MESH,
         )
         copy.start()
-        ag_copies[p, i, e] = copy
-
-    def ag_wait(p, i, e):
-        if (p, i, e) not in ag_done:
-            ag_done.add((p, i, e))
-            ag_copies[p, i, e].wait_recv()
+        ag_copies[p, i, e, h] = copy
+
+    def ag_wait(p, i, e, h):
+        if (p, i, e, h) not in ag_done:
+            ag_done.add((p, i, e, h))
+            ag_copies[p, i, e, h].wait_recv()
 
     for i in range(stages):
         for p in range(2):
-            ag_send(p, i, 0)
-
-    for copy in meta_copies:
-        copy.wait_recv()
-    full = jnp.zeros((8, 128), jnp.int32)
-    for x in range(n):
-        full = jnp.where(lane // maxb == x, meta_v[x], full)
-    full_v[...] = full
-    to_smem = pltpu.make_async_copy(full_v, full_s, in_sem.at[3])
-    to_smem.start()
-
-    wide = lax.broadcasted_iota(jnp.int32, (slots, 128), 1)
-    tall = lax.broadcasted_iota(jnp.int32, (slots, 128), 0)
-    alive = lax.rem(lane[0:1], maxb) < full[2:3]
-    table = jnp.full((8, 128), slots, jnp.int32)
-    for k in range(2):
-        named = jnp.broadcast_to(jnp.where(alive, full[k:k + 1], -1), (slots, 128))
-        named_t = jnp.sum(jnp.where(wide == tall, named, 0), axis=1, keepdims=True)
-        before = jnp.max(
-            jnp.where((named_t == named) & (tall < wide), tall, -1), axis=0, keepdims=True
-        )
-        last = jnp.max(jnp.where(named_t == wide, tall, -1), axis=0, keepdims=True)
-        table = jnp.where(sub == k, jnp.where(before < 0, slots, before), table)
-        table = jnp.where(sub == 2 + k, jnp.where(last < 0, slots, last), table)
-    table_out[...] = table
-    table_copy = pltpu.make_async_copy(table_out, table_s, in_sem.at[4])
-    table_copy.start()
-    to_smem.wait()
-    pltpu.make_async_copy(cot_v, cot_v, in_sem.at[1]).wait()
-    pltpu.make_async_copy(hid_v, hid_v, in_sem.at[0]).wait()
-
-    def term(q):
+            for h in range(2):
+                if h == 0 or i == 0 or i == chip_bits:
+                    ag_send(p, i, 0, h)
+
+    def collect(xs, full):
+        for x in xs:
+            if x:
+                meta_copies[x - 1].wait_recv()
+            full = jnp.where(lane // maxb == place[x], meta_v[x], full)
+        return full
+
+    def to_smem(k):
+        return pltpu.make_async_copy(full_v.at[k], full_s.at[k], in_sem.at[3 + k])
+
+    known = collect(near, jnp.zeros((8, 128), jnp.int32))
+    full_v[0] = known
+    to_smem(0).start()
+
+    def term(x, j):
+        k = 0 if x in near else 1
+        q = place[x] * maxb + j
         return lax.dot_general(
-            hid_v[full_s[0, q]], cot_v[full_s[1, q]],
+            hid_v[full_s[k, 0, q]], cot_v[full_s[k, 1, q]],
             (((0,), (0,)), ((), ())), preferred_element_type=F32,
         )
 
@@ -531,42 +526,66 @@
     for t in range(stages):
         offsets.append(offsets[-1] + (n >> (t + 1)))
 
+    def pair_copy(p, e):
+        return pltpu.make_async_remote_copy(
+            sbuf.at[p, e], rbuf.at[p, e], rs_ss.at[p, e, 0], rs_rs.at[p, e, 0],
+            device_id={"fsdp": relative(1)}, device_id_type=MESH,
+        )
+
     def rs_copy(p, t, e, c):
         where = offsets[t] + e
-        bit = 0 if t == 0 else orders[p][t - 1]
         return pltpu.make_async_remote_copy(
             sbuf.at[p, where, c], rbuf.at[p, where, c],
             rs_ss.at[p, where, c], rs_rs.at[p, where, c],
-            device_id={"fsdp": relative(1 << bit)}, device_id_type=MESH,
-        )
-
-    def foreign(c):
-        for e in range(chips):
-            for p in range(2):
-                q = (owner_at(p, e) | 1) * maxb + p * half + c
-                sbuf[p, e, c] = term(q).astype(BF16)
-                rs_copy(p, 0, e, c).start()
-
-    def own(c):
-        for e in range(chips):
-            for p in range(2):
-                acc[p, e, c] = term(owner_at(p, e) * maxb + p * half + c)
+            device_id={"fsdp": relative(1 << orders[p][t - 1])}, device_id_type=MESH,
+        )
+
+    def foreign(e):
+        for p in range(2):
+            for c in range(half):
+                sbuf[p, e, c] = term(owner_at(p, e) | 1, p * half + c).astype(BF16)
+        for p in range(2):
+            pair_copy(p, e).start()
+
+    def own(e):
+        for p in range(2):
+            for c in range(half):
+                acc[p, e, c] = term(owner_at(p, e), p * half + c)
 
     starts = [0]
     for t in range(stages):
         starts.append(starts[-1] + (n >> (t + 1)) // 2)
+
+    paired = set()
+
+    def pair_wait(p, e):
+        if (p, e) not in paired:
+            paired.add((p, e))
+            pair_copy(p, e).wait_recv()
+
+    def pass_on(e, cs):
+        for p in range(2):
+            pair_wait(p, e)
+            for c in cs:
+                total = acc[p, e, c] + rbuf[p, e, c].astype(F32)
+                sbuf[p, offsets[1] + e, c] = total.astype(BF16)
+            for c in cs:
+                rs_copy(p, 1, e, c).start()
 
     def reduce_step(t, c):
         m = n >> (t + 1)
         for e in range(m):
             for p in range(2):
+                at_e = starts[t] + e
                 rs_copy(p, t, e, c).wait_recv()
-                total = acc[p, starts[t] + e, c] + rbuf[p, offsets[t] + e, c].astype(F32)
+                total = acc[p, at_e, c] + rbuf[p, offsets[t] + e, c].astype(F32)
+                if t == 1:
+                    total = total + rbuf[p, at_e, c].astype(F32)
                 if e < m // 2:
                     sbuf[p, offsets[t + 1] + e, c] = total.astype(BF16)
                     rs_copy(p, t + 1, e, c).start()
                 elif m > 1:
-                    acc[p, starts[t] + e, c] = total
+                    acc[p, at_e, c] = total
                 else:
                     at = pl.ds(p * edge, edge)
                     fin[c, at] = total
@@ -603,14 +622,14 @@
             a_copy(c, r).start()
         return squares + jnp.sum((piece * piece).reshape(-1, 8, 128), axis=0)
 
-    def project(x):
+    def project(at):
         def load(j):
-            q = x * maxb + j
+            q = at * maxb + j
             backward = lax.dot_general(
-                cot_v[full_s[1, q]], tiles_v[x, j], (((1,), (1,)), ((), ())),
+                cot_v[full_s[1, 1, q]], tiles_v[at, j], (((1,), (1,)), ((), ())),
                 preferred_element_type=F32,
             )
-            forward = jnp.dot(hid_v[full_s[0, q]], tiles_v[x, j], preferred_element_type=F32)
+            forward = jnp.dot(hid_v[full_s[1, 0, q]], tiles_v[at, j], preferred_element_type=F32)
             return q, backward, forward
         for j in range(maxb):
             q, backward, forward = load(j)
@@ -627,82 +646,129 @@
             index = [t for t in range(stages) if (x >> bits[t]) & 1]
             if index:
                 e = sum(1 << t for t in index[:-1])
-                ag_wait(p, index[-1], e)
-
-    foreign(0)
-
-    def first(c, carry):
-        @pl.when(c + 1 < half)
-        def _():
-            foreign(c + 1)
-        own(c)
-        reduce_step(0, c)
+                for h in range(2):
+                    ag_wait(p, index[-1], e, h)
+
+    sent = sorted(range(chips // 2), key=lambda e: bin(owner_at(0, e)).count("1"))
+    kept = list(range(chips // 2, chips))
+    to_smem(0).wait()
+    pltpu.make_async_copy(cot_v, cot_v, in_sem.at[1]).wait()
+    pltpu.make_async_copy(hid_v, hid_v, in_sem.at[0]).wait()
+    foreign(sent[0])
+    full = collect(far, known)
+    full_v[1] = full
+    to_smem(1).start()
+    own(sent[0])
+    to_smem(1).wait()
+    lead, middle, tail = range(half // 2), range(half // 2, half - 1), [half - 1]
+    for k in range(1, len(sent)):
+        foreign(sent[k])
+        pass_on(sent[k - 1], lead)
+        own(sent[k])
+    for e in kept:
+        foreign(e)
+    pass_on(sent[-1], lead)
+    for e in sent:
+        pass_on(e, middle)
+
+    wide = lax.broadcasted_iota(jnp.int32, (slots, 128), 1)
+    tall = lax.broadcasted_iota(jnp.int32, (slots, 128), 0)
+    alive = lax.rem(lane[0:1], maxb) < full[2:3]
+    table = jnp.full((8, 128), slots, jnp.int32)
+    for k in range(2):
+        named = jnp.broadcast_to(jnp.where(alive, full[k:k + 1], -1), (slots, 128))
+        named_t = jnp.sum(jnp.where(wide == tall, named, 0), axis=1, keepdims=True)
+        before = jnp.max(
+            jnp.where((named_t == named) & (tall < wide), tall, -1), axis=0, keepdims=True
+        )
+        last = jnp.max(jnp.where(named_t == wide, tall, -1), axis=0, keepdims=True)
+        table = jnp.where(sub == k, jnp.where(before < 0, slots, before), table)
+        table = jnp.where(sub == 2 + k, jnp.where(last < 0, slots, last), table)
+    table_out[...] = table
+    table_copy = pltpu.make_async_copy(table_out, table_s, in_sem.at[7])
+    table_copy.start()
+    for e in kept:
+        own(e)
+    table_copy.wait()
+
+    def project_all(xs):
+        for x in xs:
+            arrived(x)
+        first = place[xs[0]]
+
+        def one(at, carry):
+            project(at)
+            return carry
+
+        lax.fori_loop(first, first + len(xs), one, 0)
+
+    def ag_pass(i, e, h):
+        for p in range(2):
+            ag_wait(p, i, e, h)
+            ag_send(p, chip_bits, e + 2 ** i, h)
+
+    project_all([0, 1])
+    for h in range(2):
+        for i in range(chip_bits if h == 0 else 1):
+            ag_pass(i, 0, h)
+    for e in kept:
+        for p in range(2):
+            pair_wait(p, e)
+    reduce_step(1, 0)
+    for e in sent:
+        pass_on(e, tail)
+
+    def second(c, carry):
+        reduce_step(1, c)
         return carry
 
-    lax.fori_loop(0, half, first, 0)
-
-    for i in range(chip_bits):
-        for p in range(2):
-            ag_wait(p, i, 0)
-            ag_send(p, chip_bits, 2 ** i)
-    table_copy.wait()
-    early = [x for x in range(n) if bin(x >> 1).count("1") < 2]
-    for x in early:
-        arrived(x)
-
-    def second(k, carry):
-        project(k)
-        reduce_step(1, k)
-        return carry
-
-    lax.fori_loop(0, half, second, 0)
+    lax.fori_loop(1, half, second, 0)
+
     for i in range(1, chip_bits):
         for p in range(2):
-            for e in range(1, 2 ** i):
-                ag_wait(p, i - 1, e - 2 ** (i - 1))
-                ag_send(p, i, e)
-
-    def third(k, carry):
-        @pl.when(half + k < len(early))
-        def _():
-            project(half + k)
-        reduce_step(2, k)
-        return carry
-
-    lax.fori_loop(0, half, third, 0)
-
+            ag_send(p, i, 0, 1)
     for i in range(1, chip_bits):
-        for p in range(2):
-            for e in range(1, 2 ** i):
-                ag_wait(p, i, e)
-                ag_send(p, chip_bits, e + 2 ** i)
-
-    squares = lax.fori_loop(0, half, z_step, jnp.zeros((8, 128), F32))
-    place = me * dp + z
-    sqf[place] = jnp.sum(squares, axis=0, keepdims=True)
+        for e in range(1, 2 ** i):
+            for p in range(2):
+                for h in range(2):
+                    ag_wait(p, i - 1, e - 2 ** (i - 1), h)
+                    ag_send(p, i, e, h)
+
+    for t in range(2, stages):
+        def third(c, carry):
+            reduce_step(t, c)
+            return carry
+
+        lax.fori_loop(0, half, third, 0)
+
+    for i in range(1, chip_bits):
+        ag_pass(i, 0, 1)
+    project_all([x for x in near if x > 1 and x % 2 == 0])
+    squares = lax.fori_loop(0, half // 2, z_step, jnp.zeros((8, 128), F32))
+    project_all([x for x in near if x > 1 and x % 2 == 1])
+    for i in range(1, chip_bits):
+        for e in range(1, 2 ** i):
+            for h in range(2):
+                ag_pass(i, e, h)
+    squares = lax.fori_loop(half // 2, half, z_step, squares)
+    device = me * dp + z
+    sqf[device] = jnp.sum(squares, axis=0, keepdims=True)
     sq_copies = []
     for x in range(n):
         for r in range(dp):
             if x or r:
                 copy = pltpu.make_async_remote_copy(
-                    sqf.at[place], sqf.at[place], sq_ss, sq_rs,
+                    sqf.at[device], sqf.at[device], sq_ss, sq_rs,
                     device_id={"fsdp": relative(x), "dp": z_peer(r)}, device_id_type=MESH,
                 )
                 copy.start()
                 sq_copies.append(copy)
 
-    for x in range(len(early), n):
-        arrived(x)
-
-    def rest(x, carry):
-        project(x)
-        return carry
-
-    lax.fori_loop(len(early), n, rest, 0)
-
-    entries = full_s[2, 0]
+    project_all(far)
+
+    entries = full_s[1, 2, 0]
     for x in range(1, n):
-        entries = entries + full_s[2, x * maxb]
+        entries = entries + full_s[1, 2, x * maxb]
     others = sqf.at[pl.ds(0, n * dp - 1)]
     pltpu.make_async_copy(others, others, sq_rs).wait()
     squares = jnp.sum(jnp.sum(sqf[...], axis=0), axis=1, keepdims=True)
@@ -723,8 +789,12 @@
         copy.wait_send()
     pltpu.make_async_copy(others, others, sq_ss).wait()
 
+    for e in range(chips):
+        for p in range(2):
+            pair_copy(p, e).wait_send()
+
     def drain(c, carry):
-        for t in range(stages):
+        for t in range(1, stages):
             for e in range(n >> (t + 1)):
                 for p in range(2):
                     rs_copy(p, t, e, c).wait_send()
@@ -792,8 +862,8 @@
             pltpu.VMEM((blocks_model, tokens, edge), BF16),
             pltpu.VMEM((n, maxb, edge, edge), BF16),
             pltpu.VMEM((n, 8, 128), jnp.int32),
-            pltpu.VMEM((8, 128), jnp.int32),
-            pltpu.SMEM((8, 128), jnp.int32),
+            pltpu.VMEM((2, 8, 128), jnp.int32),
+            pltpu.SMEM((2, 8, 128), jnp.int32),
             pltpu.SMEM((8, 128), jnp.int32),
             pltpu.VMEM((2, n // 2, half, edge, edge), F32),
             pltpu.VMEM((2, n - 1, half, edge, edge), BF16),
@@ -805,9 +875,9 @@
             pltpu.VMEM((n * dp, 1, 128), F32),
             pltpu.VMEM((slots + 1, tokens, edge), F32),
             pltpu.VMEM((slots + 1, tokens, edge), F32),
-            dma((7,)),
+            dma((8,)),
             dma((n - 1,)), dma((n - 1,)),
-            dma((2, n - 1)), dma((2, n - 1)),
+            dma((2, n - 1, 2)), dma((2, n - 1, 2)),
             dma((2, n - 1, half)), dma((2, n - 1, half)),
             dma((half, dp - 1)), dma((half, dp - 1)),
             dma((half, dp - 1)), dma((half, dp - 1)),

time: 45.3 us -> 41.6 us (0.918)
  Pallas kernels: 43.9 us -> 40.2 us
    pallas_call x1, Pallas kernels: 39.7 us -> 36 us  [fused(): pl.pallas_call(functools.partial(fused_kernel, n, dp, root), out_shape=(p...]
where the time goes in v3:
time: 41.6 us; the launch traced here: 41.5 us
  Pallas kernels  40.2 us (97%)
  between operations  1.29 us (3%)
    pallas_call x1, Pallas kernels, fused(): pl.pallas_call(functools.partial(fused_kernel, n, dp, root), out_shape=(p...  36 us
    pallas_call x1, Pallas kernels, fused(): pl.pallas_call(write_kernel, out_shape=(jax.ShapeDtypeStruct(cotangent.sh...  4.15 us

profile of v3, /device:TPU:0, one launch (start us, length us, event | category | flops | bytes accessed | tf_op | source)
XLA Modules:
  0.0 41.5 jit_solution(13088909145153081944)
XLA Ops:
  1.3 36.0 %fused.1 = (bf16[65,256,128]{2,1,0:T(8,128)(2,1)S(1)}, bf16[65,256,128]{2,1,0:T(8,128)(2,1)S(1)}, f32[8,128,128]{2,1,0:T(8,128)S(1)}, s32[8,128]{1,0:T(8,128)S(1)}) custom-call(s32[8]{0:T(128)} %rows_hbm.1, s32[8]{0:T(128)} %cols_hbm.1, s32[1]{0:T(128)S(6)} %copy.9.cnt_s, bf16[8,128,128]{2,1,0:T(8,128)(2,1)} %tiles_hbm.1, bf16[256,14336]{1,0:T(8,128)(2,1)} %hid_hbm.1, ...), custom_call_target="tpu_custom_call" | custom-call | tf_op jit(solution)/shard_map/fused/pallas_call | solution.py:848
  37.3 4.1 %write.1 = (bf16[256,4096]{1,0:T(8,128)(2,1)}, bf16[256,14336]{1,0:T(8,128)(2,1)}, f32[8,128,128]{2,1,0:T(8,128)}) custom-call(bf16[65,256,128]{2,1,0:T(8,128)(2,1)S(1)} %get-tuple-element.7.grad_v, bf16[65,256,128]{2,1,0:T(8,128)(2,1)S(1)} %get-tuple-element.8.layer_v, f32[8,128,128]{2,1,0:T(8,128)S(1)} %get-tuple-element.9.wg_v, ...), custom_call_target="tpu_custom_call" | custom-call | tf_op jit(solution)/shard_map/write/pallas_call | solution.py:891

commit v4 on v3

--- a/solution.py
+++ b/solution.py
@@ -376,11 +376,10 @@
 def fused_kernel(
     n, dp, root,
     rows_hbm, cols_hbm, cnt_s, tiles_hbm, hid_hbm, cot_hbm,
-    grad_out, layer_out, wg_out, table_out,
-    rows_s, cols_s, hid_v, cot_v, tiles_v, meta_v, full_v, full_s, table_s,
+    grad_out, layer_out, wg_out, table_s,
+    rows_s, cols_s, hid_v, cot_v, tiles_v, meta_v, full_v, full_s, table_v,
     acc, sbuf, rbuf, fin, zs, zr, za, sqf, grad_q, layer_q,
-    in_sem, meta_ss, meta_rs, ag_ss, ag_rs, rs_ss, rs_rs,
-    zs_ss, zs_rs, za_ss, za_rs, sq_ss, sq_rs,
+    in_sem, send_sem, meta_rs, ag_rs, pair_rs, rs_rs, z_rs, za_rs, sq_rs,
 ):
     me = lax.axis_index("fsdp")
     z = lax.axis_index("dp")
@@ -412,30 +411,39 @@
     queue += [x for x in near if x > 1 and x % 2 == 1] + far
     place = [queue.index(x) for x in range(n)]
 
-    def fetch(source, target, sem):
+    def fetch(source, target, sem, first, last):
         def step(i, carry):
             at = pl.ds(pl.multiple_of(i * edge, edge), edge)
             pltpu.make_async_copy(source.at[:, at], target.at[i], sem).start()
             return carry
-        lax.fori_loop(0, target.shape[0], step, 0)
-
-    rows_copy = pltpu.make_async_copy(rows_hbm, rows_s, in_sem.at[5])
-    rows_copy.start()
-    cols_copy = pltpu.make_async_copy(cols_hbm, cols_s, in_sem.at[6])
-    cols_copy.start()
-    own_copy = pltpu.make_async_copy(tiles_hbm, tiles_v.at[0], in_sem.at[2])
-    own_copy.start()
+        lax.fori_loop(first, last, step, 0)
+
+    def blocks_wait(count, sem):
+        if count <= maxb:
+            blocks = tiles_v.at[0, pl.ds(0, count)]
+        else:
+            blocks = tiles_v.at[pl.ds(0, count // maxb)]
+        pltpu.make_async_copy(blocks, blocks, sem).wait()
+
     barrier = pltpu.get_barrier_semaphore()
-    for x in range(1, n):
-        pl.semaphore_signal(
-            barrier, inc=1, device_id={"fsdp": relative(x)}, device_id_type=MESH
-        )
     for r in range(1, dp):
         pl.semaphore_signal(
             barrier, inc=1, device_id={"dp": z_peer(r)}, device_id_type=MESH
         )
-    fetch(cot_hbm, cot_v, in_sem.at[1])
-    fetch(hid_hbm, hid_v, in_sem.at[0])
+    for x in range(n - 1, 0, -1):
+        pl.semaphore_signal(
+            barrier, inc=1, device_id={"fsdp": relative(x)}, device_id_type=MESH
+        )
+    rows_copy = pltpu.make_async_copy(rows_hbm, rows_s, in_sem.at[2])
+    rows_copy.start()
+    cols_copy = pltpu.make_async_copy(cols_hbm, cols_s, in_sem.at[3])
+    cols_copy.start()
+    own_copy = pltpu.make_async_copy(tiles_hbm, tiles_v.at[0], in_sem.at[7])
+    own_copy.start()
+
+    early = hid_v.shape[0] * 3 // 8
+    fetch(cot_hbm, cot_v, in_sem.at[1], 0, cot_v.shape[0])
+    fetch(hid_hbm, hid_v, in_sem.at[0], 0, early)
 
     lane = lax.broadcasted_iota(jnp.int32, (8, 128), 1)
     sub = lax.broadcasted_iota(jnp.int32, (8, 128), 0)
@@ -447,24 +455,22 @@
         meta = jnp.where((sub == 0) & here, rows_s[j], meta)
         meta = jnp.where((sub == 1) & here, cols_s[j], meta)
     meta_v[0] = meta
-    grad_q[slots] = jnp.zeros(grad_q.shape[1:], F32)
-    layer_q[slots] = jnp.zeros(layer_q.shape[1:], F32)
-    grad_out[slots] = jnp.zeros(grad_out.shape[1:], BF16)
-    layer_out[slots] = jnp.zeros(layer_out.shape[1:], BF16)
+    pl.semaphore_wait(barrier, n - 1 + dp - 1)
+
+    for x in range(n - 1, 0, -1):
+        pltpu.make_async_remote_copy(
+            meta_v.at[0], meta_v.at[place[x]], send_sem.at[0], meta_rs.at[int(x in far)],
+            device_id={"fsdp": relative(x)}, device_id_type=MESH,
+        ).start()
     own_copy.wait()
-    pl.semaphore_wait(barrier, n - 1 + dp - 1)
-
-    meta_copies = []
-    for x in range(1, n):
-        copy = pltpu.make_async_remote_copy(
-            meta_v.at[0], meta_v.at[x], meta_ss.at[x - 1], meta_rs.at[x - 1],
-            device_id={"fsdp": relative(x)}, device_id_type=MESH,
-        )
-        copy.start()
-        meta_copies.append(copy)
-
-    ag_copies = {}
+
     ag_done = set()
+
+    def ag_index(i, e, h):
+        split = 0 < i < chip_bits and e == 0
+        keys = [(i, e, h) for i in range(stages) for e in range(2 ** i) for h in range(2)
+                if h == 0 or (0 < i < chip_bits and e == 0)]
+        return keys.index((i, e, h if split else 0)), maxb // 2 if split else maxb
 
     def ag_send(p, i, e, h):
         bits = orders[p] + [0]
@@ -472,20 +478,18 @@
         for t in range(len(bits)):
             if (e >> t) & 1:
                 owner |= 1 << bits[t]
-        where = 2 ** i - 1 + e
         part = pl.ds(p * half + h * (half // 2), half // 2)
-        copy = pltpu.make_async_remote_copy(
+        pltpu.make_async_remote_copy(
             tiles_v.at[place[owner], part], tiles_v.at[place[owner | (1 << bits[i])], part],
-            ag_ss.at[p, where, h], ag_rs.at[p, where, h],
+            send_sem.at[1], ag_rs.at[ag_index(i, e, h)[0]],
             device_id={"fsdp": relative(1 << bits[i])}, device_id_type=MESH,
-        )
-        copy.start()
-        ag_copies[p, i, e, h] = copy
-
-    def ag_wait(p, i, e, h):
-        if (p, i, e, h) not in ag_done:
-            ag_done.add((p, i, e, h))
-            ag_copies[p, i, e, h].wait_recv()
+        ).start()
+
+    def ag_wait(i, e, h):
+        index, count = ag_index(i, e, h)
+        if index not in ag_done:
+            ag_done.add(index)
+            blocks_wait(count, ag_rs.at[index])
 
     for i in range(stages):
         for p in range(2):
@@ -493,15 +497,24 @@
                 if h == 0 or i == 0 or i == chip_bits:
                     ag_send(p, i, 0, h)
 
+    grad_q[slots] = jnp.zeros(grad_q.shape[1:], F32)
+    layer_q[slots] = jnp.zeros(layer_q.shape[1:], F32)
+    grad_out[slots] = jnp.zeros(grad_out.shape[1:], BF16)
+    layer_out[slots] = jnp.zeros(layer_out.shape[1:], BF16)
+
+    fetch(hid_hbm, hid_v, in_sem.at[0], early, hid_v.shape[0])
+
     def collect(xs, full):
+        arrive = [x for x in xs if x]
+        first = min(place[x] for x in arrive)
+        metas = meta_v.at[pl.ds(first, len(arrive))]
+        pltpu.make_async_copy(metas, metas, meta_rs.at[int(xs is far)]).wait()
         for x in xs:
-            if x:
-                meta_copies[x - 1].wait_recv()
-            full = jnp.where(lane // maxb == place[x], meta_v[x], full)
+            full = jnp.where(lane // maxb == place[x], meta_v[place[x]], full)
         return full
 
     def to_smem(k):
-        return pltpu.make_async_copy(full_v.at[k], full_s.at[k], in_sem.at[3 + k])
+        return pltpu.make_async_copy(full_v.at[k], full_s.at[k], in_sem.at[4 + k])
 
     known = collect(near, jnp.zeros((8, 128), jnp.int32))
     full_v[0] = known
@@ -528,7 +541,7 @@
 
     def pair_copy(p, e):
         return pltpu.make_async_remote_copy(
-            sbuf.at[p, e], rbuf.at[p, e], rs_ss.at[p, e, 0], rs_rs.at[p, e, 0],
+            sbuf.at[p, e], rbuf.at[p, e], send_sem.at[2], pair_rs.at[e],
             device_id={"fsdp": relative(1)}, device_id_type=MESH,
         )
 
@@ -536,7 +549,7 @@
         where = offsets[t] + e
         return pltpu.make_async_remote_copy(
             sbuf.at[p, where, c], rbuf.at[p, where, c],
-            rs_ss.at[p, where, c], rs_rs.at[p, where, c],
+            send_sem.at[2], rs_rs.at[t - 1, c],
             device_id={"fsdp": relative(1 << orders[p][t - 1])}, device_id_type=MESH,
         )
 
@@ -558,14 +571,14 @@
 
     paired = set()
 
-    def pair_wait(p, e):
-        if (p, e) not in paired:
-            paired.add((p, e))
-            pair_copy(p, e).wait_recv()
+    def pair_wait(e):
+        if e not in paired:
+            paired.add(e)
+            blocks_wait(maxb, pair_rs.at[e])
 
     def pass_on(e, cs):
         for p in range(2):
-            pair_wait(p, e)
+            pair_wait(e)
             for c in cs:
                 total = acc[p, e, c] + rbuf[p, e, c].astype(F32)
                 sbuf[p, offsets[1] + e, c] = total.astype(BF16)
@@ -574,10 +587,10 @@
 
     def reduce_step(t, c):
         m = n >> (t + 1)
+        blocks_wait(2 * m, rs_rs.at[t - 1, c])
         for e in range(m):
             for p in range(2):
                 at_e = starts[t] + e
-                rs_copy(p, t, e, c).wait_recv()
                 total = acc[p, at_e, c] + rbuf[p, offsets[t] + e, c].astype(F32)
                 if t == 1:
                     total = total + rbuf[p, at_e, c].astype(F32)
@@ -599,20 +612,20 @@
 
     def z_copy(c, r):
         return pltpu.make_async_remote_copy(
-            zs.at[c, z_rows(z_peer(r))], zr.at[c, r - 1], zs_ss.at[c, r - 1], zs_rs.at[c, r - 1],
+            zs.at[c, z_rows(z_peer(r))], zr.at[c, r - 1], send_sem.at[3], z_rs.at[c],
             device_id={"dp": z_peer(r)}, device_id_type=MESH,
         )
 
     def a_copy(c, r):
         return pltpu.make_async_remote_copy(
-            za.at[c, z_rows(z)], za.at[c, z_rows(z)], za_ss.at[c, r - 1], za_rs.at[c, r - 1],
+            za.at[c, z_rows(z)], za.at[c, z_rows(z)], send_sem.at[4], za_rs,
             device_id={"dp": z_peer(r)}, device_id_type=MESH,
         )
 
     def z_step(c, squares):
         piece = fin[c, z_rows(z)]
+        pltpu.make_async_copy(zr.at[c], zr.at[c], z_rs.at[c]).wait()
         for r in range(1, dp):
-            z_copy(c, r).wait_recv()
             piece = piece + zr[c, r - 1].astype(F32)
         row = z * rows_z + lax.broadcasted_iota(jnp.int32, piece.shape, 0)
         slot = (row // edge) * half + c
@@ -647,7 +660,7 @@
             if index:
                 e = sum(1 << t for t in index[:-1])
                 for h in range(2):
-                    ag_wait(p, index[-1], e, h)
+                    ag_wait(index[-1], e, h)
 
     sent = sorted(range(chips // 2), key=lambda e: bin(owner_at(0, e)).count("1"))
     kept = list(range(chips // 2, chips))
@@ -660,16 +673,17 @@
     to_smem(1).start()
     own(sent[0])
     to_smem(1).wait()
-    lead, middle, tail = range(half // 2), range(half // 2, half - 1), [half - 1]
     for k in range(1, len(sent)):
         foreign(sent[k])
-        pass_on(sent[k - 1], lead)
+        pass_on(sent[k - 1], [0])
         own(sent[k])
-    for e in kept:
+    foreign(kept[0])
+    pass_on(sent[-1], [0])
+    for c in range(1, half - 1):
+        for e in sent:
+            pass_on(e, [c])
+    for e in kept[1:]:
         foreign(e)
-    pass_on(sent[-1], lead)
-    for e in sent:
-        pass_on(e, middle)
 
     wide = lax.broadcasted_iota(jnp.int32, (slots, 128), 1)
     tall = lax.broadcasted_iota(jnp.int32, (slots, 128), 0)
@@ -684,8 +698,8 @@
         last = jnp.max(jnp.where(named_t == wide, tall, -1), axis=0, keepdims=True)
         table = jnp.where(sub == k, jnp.where(before < 0, slots, before), table)
         table = jnp.where(sub == 2 + k, jnp.where(last < 0, slots, last), table)
-    table_out[...] = table
-    table_copy = pltpu.make_async_copy(table_out, table_s, in_sem.at[7])
+    table_v[...] = table
+    table_copy = pltpu.make_async_copy(table_v, table_s, in_sem.at[6])
     table_copy.start()
     for e in kept:
         own(e)
@@ -703,8 +717,8 @@
         lax.fori_loop(first, first + len(xs), one, 0)
 
     def ag_pass(i, e, h):
-        for p in range(2):
-            ag_wait(p, i, e, h)
+        ag_wait(i, e, h)
+        for p in range(2):
             ag_send(p, chip_bits, e + 2 ** i, h)
 
     project_all([0, 1])
@@ -712,17 +726,25 @@
         for i in range(chip_bits if h == 0 else 1):
             ag_pass(i, 0, h)
     for e in kept:
-        for p in range(2):
-            pair_wait(p, e)
+        pair_wait(e)
     reduce_step(1, 0)
     for e in sent:
-        pass_on(e, tail)
+        pass_on(e, [half - 1])
 
     def second(c, carry):
         reduce_step(1, c)
         return carry
 
-    lax.fori_loop(1, half, second, 0)
+    lax.fori_loop(1, half - 1, second, 0)
+    for t in range(2, stages):
+        reduce_step(t, 0)
+    reduce_step(1, half - 1)
+    for t in range(2, stages):
+        def third(c, carry):
+            reduce_step(t, c)
+            return carry
+
+        lax.fori_loop(1, half, third, 0)
 
     for i in range(1, chip_bits):
         for p in range(2):
@@ -731,39 +753,29 @@
         for e in range(1, 2 ** i):
             for p in range(2):
                 for h in range(2):
-                    ag_wait(p, i - 1, e - 2 ** (i - 1), h)
+                    ag_wait(i - 1, e - 2 ** (i - 1), h)
                     ag_send(p, i, e, h)
 
-    for t in range(2, stages):
-        def third(c, carry):
-            reduce_step(t, c)
-            return carry
-
-        lax.fori_loop(0, half, third, 0)
-
+    squares = lax.fori_loop(0, half // 2, z_step, jnp.zeros((8, 128), F32))
     for i in range(1, chip_bits):
         ag_pass(i, 0, 1)
     project_all([x for x in near if x > 1 and x % 2 == 0])
-    squares = lax.fori_loop(0, half // 2, z_step, jnp.zeros((8, 128), F32))
+    squares = lax.fori_loop(half // 2, half, z_step, squares)
+    device = me * dp + z
+    sqf[device] = jnp.sum(squares, axis=0, keepdims=True)
+    for x in range(n):
+        for r in range(dp):
+            if x or r:
+                pltpu.make_async_remote_copy(
+                    sqf.at[device], sqf.at[device], send_sem.at[5], sq_rs,
+                    device_id={"fsdp": relative(x), "dp": z_peer(r)}, device_id_type=MESH,
+                ).start()
+
     project_all([x for x in near if x > 1 and x % 2 == 1])
     for i in range(1, chip_bits):
         for e in range(1, 2 ** i):
             for h in range(2):
                 ag_pass(i, e, h)
-    squares = lax.fori_loop(half // 2, half, z_step, squares)
-    device = me * dp + z
-    sqf[device] = jnp.sum(squares, axis=0, keepdims=True)
-    sq_copies = []
-    for x in range(n):
-        for r in range(dp):
-            if x or r:
-                copy = pltpu.make_async_remote_copy(
-                    sqf.at[device], sqf.at[device], sq_ss, sq_rs,
-                    device_id={"fsdp": relative(x), "dp": z_peer(r)}, device_id_type=MESH,
-                )
-                copy.start()
-                sq_copies.append(copy)
-
     project_all(far)
 
     entries = full_s[1, 2, 0]
@@ -776,47 +788,27 @@
     spread = jnp.sqrt(squares / live)
     factor = jnp.minimum(1.0, 0.5 * root / spread) / root
 
+    pltpu.make_async_copy(zr, zr, za_rs).wait()
+
     def finish(c, carry):
-        for r in range(1, dp):
-            a_copy(c, r).wait_recv()
         for p in range(2):
             wg_out[p * half + c] = za[c, pl.ds(p * edge, edge)].astype(F32) * factor
         return carry
 
     lax.fori_loop(0, half, finish, 0)
 
-    for copy in meta_copies + list(ag_copies.values()):
-        copy.wait_send()
-    pltpu.make_async_copy(others, others, sq_ss).wait()
-
-    for e in range(chips):
-        for p in range(2):
-            pair_copy(p, e).wait_send()
-
-    def drain(c, carry):
-        for t in range(1, stages):
-            for e in range(n >> (t + 1)):
-                for p in range(2):
-                    rs_copy(p, t, e, c).wait_send()
-        for r in range(1, dp):
-            z_copy(c, r).wait_send()
-            a_copy(c, r).wait_send()
-        return carry
-
-    lax.fori_loop(0, half, drain, 0)
+    metas = meta_v.at[pl.ds(1, n - 1)]
+    gathered = tiles_v.at[pl.ds(1, n - 1)]
+    for k, sent in enumerate((metas, gathered, sbuf, zr, zr, others)):
+        pltpu.make_async_copy(sent, sent, send_sem.at[k]).wait()
 
 
 def write_kernel(
-    grad_v, layer_v, wg_v, table_v,
+    grad_v, layer_v, wg_v, table_s,
     layer_hbm, grad_hbm, wg_hbm,
-    table_s, t_sem, w_sem, g_sem, l_sem,
+    w_sem, g_sem, l_sem,
 ):
     edge = grad_v.shape[2]
-    table_copy = pltpu.make_async_copy(table_v, table_s, t_sem)
-    table_copy.start()
-    wg_copy = pltpu.make_async_copy(wg_v, wg_hbm, w_sem)
-    wg_copy.start()
-    table_copy.wait()
 
     def write(row, source, target, sem):
         def step(i, carry):
@@ -827,6 +819,8 @@
 
     write(2, grad_v, grad_hbm, g_sem)
     write(3, layer_v, layer_hbm, l_sem)
+    wg_copy = pltpu.make_async_copy(wg_v, wg_hbm, w_sem)
+    wg_copy.start()
     pltpu.make_async_copy(grad_hbm, grad_hbm, g_sem).wait()
     pltpu.make_async_copy(layer_hbm, layer_hbm, l_sem).wait()
     wg_copy.wait()
@@ -834,11 +828,9 @@
 
 def fused(n, dp, hidden, cotangent, tiles, tile_rows, tile_cols, counts):
     tokens, width_ff = hidden.shape
-    width_model = cotangent.shape[1]
     maxb, edge, _ = tiles.shape
-    blocks_ff, blocks_model = width_ff // edge, width_model // edge
     root = math.sqrt(tokens * n * dp)
-    slots, half = n * maxb, maxb // 2
+    slots, half, stages = n * maxb, maxb // 2, n.bit_length() - 1
     in_hbm = functools.partial(pltpu.with_memory_space_constraint, memory_space=pltpu.HBM)
     rows_z = 2 * edge // dp
     hbm = pl.BlockSpec(memory_space=pltpu.HBM)
@@ -851,20 +843,20 @@
             pltpu.VMEM((slots + 1, tokens, edge), BF16),
             pltpu.VMEM((slots + 1, tokens, edge), BF16),
             pltpu.VMEM((maxb, edge, edge), F32),
-            pltpu.VMEM((8, 128), jnp.int32),
+            pltpu.SMEM((8, 128), jnp.int32),
         ),
         in_specs=[hbm, hbm, smem, hbm, hbm, hbm],
-        out_specs=(vmem, vmem, vmem, vmem),
+        out_specs=(vmem, vmem, vmem, smem),
         scratch_shapes=[
             pltpu.SMEM(tile_rows.shape, jnp.int32),
             pltpu.SMEM(tile_cols.shape, jnp.int32),
-            pltpu.VMEM((blocks_ff, tokens, edge), BF16),
-            pltpu.VMEM((blocks_model, tokens, edge), BF16),
+            pltpu.VMEM((hidden.shape[1] // edge, tokens, edge), BF16),
+            pltpu.VMEM((cotangent.shape[1] // edge, tokens, edge), BF16),
             pltpu.VMEM((n, maxb, edge, edge), BF16),
             pltpu.VMEM((n, 8, 128), jnp.int32),
             pltpu.VMEM((2, 8, 128), jnp.int32),
             pltpu.SMEM((2, 8, 128), jnp.int32),
-            pltpu.SMEM((8, 128), jnp.int32),
+            pltpu.VMEM((8, 128), jnp.int32),
             pltpu.VMEM((2, n // 2, half, edge, edge), F32),
             pltpu.VMEM((2, n - 1, half, edge, edge), BF16),
             pltpu.VMEM((2, n - 1, half, edge, edge), BF16),
@@ -875,13 +867,9 @@
             pltpu.VMEM((n * dp, 1, 128), F32),
             pltpu.VMEM((slots + 1, tokens, edge), F32),
             pltpu.VMEM((slots + 1, tokens, edge), F32),
-            dma((8,)),
-            dma((n - 1,)), dma((n - 1,)),
-            dma((2, n - 1, 2)), dma((2, n - 1, 2)),
-            dma((2, n - 1, half)), dma((2, n - 1, half)),
-            dma((half, dp - 1)), dma((half, dp - 1)),
-            dma((half, dp - 1)), dma((half, dp - 1)),
-            dma, dma,
+            dma((8,)), dma((6,)), dma((2,)),
+            dma((n - 1 + max(stages - 2, 0),)),
+            dma((n // 2,)), dma((stages - 1, half)), dma((half,)), dma, dma,
         ],
         compiler_params=pltpu.CompilerParams(
             collective_id=0, has_side_effects=True, vmem_limit_bytes=44 * 2 ** 20
@@ -895,9 +883,9 @@
             jax.ShapeDtypeStruct(hidden.shape, BF16),
             jax.ShapeDtypeStruct(tiles.shape, F32),
         ),
-        in_specs=[vmem, vmem, vmem, vmem],
+        in_specs=[vmem, vmem, vmem, smem],
         out_specs=(hbm, hbm, hbm),
-        scratch_shapes=[pltpu.SMEM((8, 128), jnp.int32), dma, dma, dma, dma],
+        scratch_shapes=[dma, dma, dma],
         compiler_params=pltpu.CompilerParams(vmem_limit_bytes=16 * 2 ** 20),
         name="write",
     )(grad, layer, weight, table)

time: 41.6 us -> 40.1 us (0.964)
  Pallas kernels: 40.2 us -> 38.7 us
    pallas_call x1, Pallas kernels: 36 us -> 34.9 us  [fused(): pl.pallas_call(functools.partial(fused_kernel, n, dp, root), out_shape=(p...]
where the time goes in v4:
time: 40.1 us; the launch traced here: 39.9 us
  Pallas kernels  38.7 us (97%)
  between operations  1.29 us (3%)
    pallas_call x1, Pallas kernels, fused(): pl.pallas_call(functools.partial(fused_kernel, n, dp, root), out_shape=(p...  34.9 us
    pallas_call x1, Pallas kernels, fused(): pl.pallas_call(write_kernel, out_shape=(jax.ShapeDtypeStruct(cotangent.sh...  3.73 us

profile of v4, /device:TPU:0, one launch (start us, length us, event | category | flops | bytes accessed | tf_op | source)
XLA Modules:
  0.0 39.9 jit_solution(10284013006801138373)
XLA Ops:
  1.3 34.9 %fused.1 = (bf16[65,256,128]{2,1,0:T(8,128)(2,1)S(1)}, bf16[65,256,128]{2,1,0:T(8,128)(2,1)S(1)}, f32[8,128,128]{2,1,0:T(8,128)S(1)}, s32[8,128]{1,0:T(8,128)S(4)}) custom-call(s32[8]{0:T(128)} %rows_hbm.1, s32[8]{0:T(128)} %cols_hbm.1, s32[1]{0:T(128)S(6)} %copy.9.cnt_s, bf16[8,128,128]{2,1,0:T(8,128)(2,1)} %tiles_hbm.1, bf16[256,14336]{1,0:T(8,128)(2,1)} %hid_hbm.1, ...), custom_call_target="tpu_custom_call" | custom-call | tf_op jit(solution)/shard_map/fused/pallas_call | solution.py:840
  36.2 3.7 %write.1 = (bf16[256,4096]{1,0:T(8,128)(2,1)}, bf16[256,14336]{1,0:T(8,128)(2,1)}, f32[8,128,128]{2,1,0:T(8,128)}) custom-call(bf16[65,256,128]{2,1,0:T(8,128)(2,1)S(1)} %get-tuple-element.7.grad_v, bf16[65,256,128]{2,1,0:T(8,128)(2,1)S(1)} %get-tuple-element.8.layer_v, f32[8,128,128]{2,1,0:T(8,128)S(1)} %get-tuple-element.9.wg_v, ...), custom_call_target="tpu_custom_call" | custom-call | tf_op jit(solution)/shard_map/write/pallas_call | solution.py:879

commit v5 on v4

--- a/solution.py
+++ b/solution.py
@@ -520,11 +520,13 @@
     full_v[0] = known
     to_smem(0).start()
 
-    def term(x, j):
+    def term(x, j, named=None):
+        q = place[x] * maxb + j
         k = 0 if x in near else 1
-        q = place[x] * maxb + j
+        row = full_s[k, 0, q] if named is None else named[0, q]
+        col = full_s[k, 1, q] if named is None else named[1, q]
         return lax.dot_general(
-            hid_v[full_s[k, 0, q]], cot_v[full_s[k, 1, q]],
+            hid_v[row], cot_v[col],
             (((0,), (0,)), ((), ())), preferred_element_type=F32,
         )
 
@@ -553,10 +555,10 @@
             device_id={"fsdp": relative(1 << orders[p][t - 1])}, device_id_type=MESH,
         )
 
-    def foreign(e):
+    def foreign(e, named=None):
         for p in range(2):
             for c in range(half):
-                sbuf[p, e, c] = term(owner_at(p, e) | 1, p * half + c).astype(BF16)
+                sbuf[p, e, c] = term(owner_at(p, e) | 1, p * half + c, named).astype(BF16)
         for p in range(2):
             pair_copy(p, e).start()
 
@@ -622,7 +624,7 @@
             device_id={"dp": z_peer(r)}, device_id_type=MESH,
         )
 
-    def z_step(c, squares):
+    def z_sum(c, squares):
         piece = fin[c, z_rows(z)]
         pltpu.make_async_copy(zr.at[c], zr.at[c], z_rs.at[c]).wait()
         for r in range(1, dp):
@@ -631,9 +633,16 @@
         slot = (row // edge) * half + c
         piece = piece * jnp.clip(cnt_s[0] - slot, 0, 1).astype(F32)
         za[c, z_rows(z)] = piece.astype(BF16)
+        return squares + jnp.sum((piece * piece).reshape(-1, 8, 128), axis=0)
+
+    def a_send(c):
         for r in range(1, dp):
             a_copy(c, r).start()
-        return squares + jnp.sum((piece * piece).reshape(-1, 8, 128), axis=0)
+
+    def z_step(c, squares):
+        squares = z_sum(c, squares)
+        a_send(c)
+        return squares
 
     def project(at):
         def load(j):
@@ -664,10 +673,10 @@
 
     sent = sorted(range(chips // 2), key=lambda e: bin(owner_at(0, e)).count("1"))
     kept = list(range(chips // 2, chips))
-    to_smem(0).wait()
     pltpu.make_async_copy(cot_v, cot_v, in_sem.at[1]).wait()
     pltpu.make_async_copy(hid_v, hid_v, in_sem.at[0]).wait()
-    foreign(sent[0])
+    foreign(sent[0], known)
+    to_smem(0).wait()
     full = collect(far, known)
     full_v[1] = full
     to_smem(1).start()
@@ -760,17 +769,18 @@
     for i in range(1, chip_bits):
         ag_pass(i, 0, 1)
     project_all([x for x in near if x > 1 and x % 2 == 0])
-    squares = lax.fori_loop(half // 2, half, z_step, squares)
+    squares = lax.fori_loop(half // 2, half - 1, z_step, squares)
+    squares = z_sum(half - 1, squares)
     device = me * dp + z
     sqf[device] = jnp.sum(squares, axis=0, keepdims=True)
-    for x in range(n):
+    for x in reversed(queue):
         for r in range(dp):
             if x or r:
                 pltpu.make_async_remote_copy(
                     sqf.at[device], sqf.at[device], send_sem.at[5], sq_rs,
                     device_id={"fsdp": relative(x), "dp": z_peer(r)}, device_id_type=MESH,
                 ).start()
-
+    a_send(half - 1)
     project_all([x for x in near if x > 1 and x % 2 == 1])
     for i in range(1, chip_bits):
         for e in range(1, 2 ** i):

time: 40.1 us -> 39.3 us (0.980)
  Pallas kernels: 38.7 us -> 37.8 us
    pallas_call x1, Pallas kernels: 34.9 us -> 34.1 us  [fused(): pl.pallas_call(functools.partial(fused_kernel, n, dp, root), out_shape=(p...]
where the time goes in v5:
time: 39.3 us; the launch traced here: 39.1 us
  Pallas kernels  37.8 us (96%)
  between operations  1.29 us (3%)
    pallas_call x1, Pallas kernels, fused(): pl.pallas_call(functools.partial(fused_kernel, n, dp, root), out_shape=(p...  34.1 us
    pallas_call x1, Pallas kernels, fused(): pl.pallas_call(write_kernel, out_shape=(jax.ShapeDtypeStruct(cotangent.sh...  3.73 us

profile of v5, /device:TPU:0, one launch (start us, length us, event | category | flops | bytes accessed | tf_op | source)
XLA Modules:
  0.0 39.1 jit_solution(12668438206804076402)
XLA Ops:
  1.3 34.1 %fused.1 = (bf16[65,256,128]{2,1,0:T(8,128)(2,1)S(1)}, bf16[65,256,128]{2,1,0:T(8,128)(2,1)S(1)}, f32[8,128,128]{2,1,0:T(8,128)S(1)}, s32[8,128]{1,0:T(8,128)S(4)}) custom-call(s32[8]{0:T(128)} %rows_hbm.1, s32[8]{0:T(128)} %cols_hbm.1, s32[1]{0:T(128)S(6)} %copy.9.cnt_s, bf16[8,128,128]{2,1,0:T(8,128)(2,1)} %tiles_hbm.1, bf16[256,14336]{1,0:T(8,128)(2,1)} %hid_hbm.1, ...), custom_call_target="tpu_custom_call" | custom-call | tf_op jit(solution)/shard_map/fused/pallas_call | solution.py:850
  35.4 3.7 %write.1 = (bf16[256,4096]{1,0:T(8,128)(2,1)}, bf16[256,14336]{1,0:T(8,128)(2,1)}, f32[8,128,128]{2,1,0:T(8,128)}) custom-call(bf16[65,256,128]{2,1,0:T(8,128)(2,1)S(1)} %get-tuple-element.7.grad_v, bf16[65,256,128]{2,1,0:T(8,128)(2,1)S(1)} %get-tuple-element.8.layer_v, f32[8,128,128]{2,1,0:T(8,128)S(1)} %get-tuple-element.9.wg_v, ...), custom_call_target="tpu_custom_call" | custom-call | tf_op jit(solution)/shard_map/write/pallas_call | solution.py:889

commit v6 on v5

--- a/solution.py
+++ b/solution.py
@@ -379,7 +379,7 @@
     grad_out, layer_out, wg_out, table_s,
     rows_s, cols_s, hid_v, cot_v, tiles_v, meta_v, full_v, full_s, table_v,
     acc, sbuf, rbuf, fin, zs, zr, za, sqf, grad_q, layer_q,
-    in_sem, send_sem, meta_rs, ag_rs, pair_rs, rs_rs, z_rs, za_rs, sq_rs,
+    in_sem, send_sem, meta_rs, ag_rs, pair_rs, rs_rs, z_rs, za_rs, zb_rs, zf_rs, sq_rs,
 ):
     me = lax.axis_index("fsdp")
     z = lax.axis_index("dp")
@@ -618,11 +618,15 @@
             device_id={"dp": z_peer(r)}, device_id_type=MESH,
         )
 
-    def a_copy(c, r):
+    def a_copy(c, piece, peer, sem):
         return pltpu.make_async_remote_copy(
-            za.at[c, z_rows(z)], za.at[c, z_rows(z)], send_sem.at[4], za_rs,
-            device_id={"dp": z_peer(r)}, device_id_type=MESH,
-        )
+            za.at[c, z_rows(piece)], za.at[c, z_rows(piece)], send_sem.at[4], sem,
+            device_id={"dp": peer}, device_id_type=MESH,
+        )
+
+    handed = half // 2 if dp == 4 else 0
+    z_near = z + 1 - 2 * lax.rem(z, 2)
+    z_far = z + 2 - 4 * lax.rem(z // 2, 2)
 
     def z_sum(c, squares):
         piece = fin[c, z_rows(z)]
@@ -637,7 +641,20 @@
 
     def a_send(c):
         for r in range(1, dp):
-            a_copy(c, r).start()
+            a_copy(c, z, z_peer(r), za_rs).start()
+
+    def a_cross(c):
+        a_copy(c, z, z_far, zf_rs.at[c]).start()
+        a_copy(c, z, z_near, zb_rs).start()
+
+    def a_hand(c):
+        a_copy(c, z, z_far, zf_rs.at[c]).wait_recv()
+        a_copy(c, z_far, z_near, zb_rs).start()
+
+    def z_cross(c, squares):
+        squares = z_sum(c, squares)
+        a_cross(c)
+        return squares
 
     def z_step(c, squares):
         squares = z_sum(c, squares)
@@ -765,7 +782,8 @@
                     ag_wait(i - 1, e - 2 ** (i - 1), h)
                     ag_send(p, i, e, h)
 
-    squares = lax.fori_loop(0, half // 2, z_step, jnp.zeros((8, 128), F32))
+    squares = lax.fori_loop(0, handed, z_cross, jnp.zeros((8, 128), F32))
+    squares = lax.fori_loop(handed, half // 2, z_step, squares)
     for i in range(1, chip_bits):
         ag_pass(i, 0, 1)
     project_all([x for x in near if x > 1 and x % 2 == 0])
@@ -781,11 +799,14 @@
                     device_id={"fsdp": relative(x), "dp": z_peer(r)}, device_id_type=MESH,
                 ).start()
     a_send(half - 1)
-    project_all([x for x in near if x > 1 and x % 2 == 1])
     for i in range(1, chip_bits):
         for e in range(1, 2 ** i):
             for h in range(2):
                 ag_pass(i, e, h)
+    crossed = [x for x in near if x > 1 and x % 2 == 1]
+    for c in range(handed):
+        a_hand(c)
+    project_all(crossed)
     project_all(far)
 
     entries = full_s[1, 2, 0]
@@ -798,7 +819,11 @@
     spread = jnp.sqrt(squares / live)
     factor = jnp.minimum(1.0, 0.5 * root / spread) / root
 
-    pltpu.make_async_copy(zr, zr, za_rs).wait()
+    if handed:
+        twice = za.at[pl.ds(0, handed)]
+        pltpu.make_async_copy(twice.at[:, pl.ds(0, 2 * rows_z)], twice.at[:, pl.ds(0, 2 * rows_z)], zb_rs).wait()
+    direct = zr.at[pl.ds(handed, half - handed)]
+    pltpu.make_async_copy(direct, direct, za_rs).wait()
 
     def finish(c, carry):
         for p in range(2):
@@ -879,7 +904,7 @@
             pltpu.VMEM((slots + 1, tokens, edge), F32),
             dma((8,)), dma((6,)), dma((2,)),
             dma((n - 1 + max(stages - 2, 0),)),
-            dma((n // 2,)), dma((stages - 1, half)), dma((half,)), dma, dma,
+            dma((n // 2,)), dma((stages - 1, half)), dma((half,)), dma, dma, dma((half,)), dma,
         ],
         compiler_params=pltpu.CompilerParams(
             collective_id=0, has_side_effects=True, vmem_limit_bytes=44 * 2 ** 20

time: 39.3 us -> 38.2 us (0.972)
  Pallas kernels: 37.8 us -> 36.7 us
    pallas_call x1, Pallas kernels: 34.1 us -> 33 us  [fused(): pl.pallas_call(functools.partial(fused_kernel, n, dp, root), out_shape=(p...]
where the time goes in v6:
time: 38.2 us; the launch traced here: 38 us
  Pallas kernels  36.7 us (96%)
  between operations  1.29 us (3%)
    pallas_call x1, Pallas kernels, fused(): pl.pallas_call(functools.partial(fused_kernel, n, dp, root), out_shape=(p...  33 us
    pallas_call x1, Pallas kernels, fused(): pl.pallas_call(write_kernel, out_shape=(jax.ShapeDtypeStruct(cotangent.sh...  3.73 us

profile of v6, /device:TPU:0, one launch (start us, length us, event | category | flops | bytes accessed | tf_op | source)
XLA Modules:
  0.0 38.0 jit_solution(6113039025903535756)
XLA Ops:
  1.3 33.0 %fused.1 = (bf16[65,256,128]{2,1,0:T(8,128)(2,1)S(1)}, bf16[65,256,128]{2,1,0:T(8,128)(2,1)S(1)}, f32[8,128,128]{2,1,0:T(8,128)S(1)}, s32[8,128]{1,0:T(8,128)S(4)}) custom-call(s32[8]{0:T(128)} %rows_hbm.1, s32[8]{0:T(128)} %cols_hbm.1, s32[1]{0:T(128)S(6)} %copy.9.cnt_s, bf16[8,128,128]{2,1,0:T(8,128)(2,1)} %tiles_hbm.1, bf16[256,14336]{1,0:T(8,128)(2,1)} %hid_hbm.1, ...), custom_call_target="tpu_custom_call" | custom-call | tf_op jit(solution)/shard_map/fused/pallas_call | solution.py:875
  34.3 3.7 %write.1 = (bf16[256,4096]{1,0:T(8,128)(2,1)}, bf16[256,14336]{1,0:T(8,128)(2,1)}, f32[8,128,128]{2,1,0:T(8,128)}) custom-call(bf16[65,256,128]{2,1,0:T(8,128)(2,1)S(1)} %get-tuple-element.7.grad_v, bf16[65,256,128]{2,1,0:T(8,128)(2,1)S(1)} %get-tuple-element.8.layer_v, f32[8,128,128]{2,1,0:T(8,128)S(1)} %get-tuple-element.9.wg_v, ...), custom_call_target="tpu_custom_call" | custom-call | tf_op jit(solution)/shard_map/write/pallas_call | solution.py:914

commit v7 on v6

--- a/solution.py
+++ b/solution.py
@@ -379,7 +379,7 @@
     grad_out, layer_out, wg_out, table_s,
     rows_s, cols_s, hid_v, cot_v, tiles_v, meta_v, full_v, full_s, table_v,
     acc, sbuf, rbuf, fin, zs, zr, za, sqf, grad_q, layer_q,
-    in_sem, send_sem, meta_rs, ag_rs, pair_rs, rs_rs, z_rs, za_rs, zb_rs, zf_rs, sq_rs,
+    in_sem, send_sem, meta_rs, ag_rs, pair_rs, rs_rs, z_rs, za_rs, zb_rs, zf_rs, sq_rs, ready,
 ):
     me = lax.axis_index("fsdp")
     z = lax.axis_index("dp")
@@ -405,6 +405,10 @@
     def z_peer(r):
         return lax.rem(z + r, dp)
 
+    z_near = z + 1 - 2 * lax.rem(z, 2)
+    z_far = z + 2 - 4 * lax.rem(z // 2, 2)
+    greeted = [z_near, z_far] if dp == 4 else [z_peer(r) for r in range(1, dp)]
+
     near = [x for x in range(n) if bin(x >> 1).count("1") < 2]
     far = [x for x in range(n) if x not in near]
     queue = [0, 1] + [x for x in near if x > 1 and x % 2 == 0]
@@ -426,10 +430,8 @@
         pltpu.make_async_copy(blocks, blocks, sem).wait()
 
     barrier = pltpu.get_barrier_semaphore()
-    for r in range(1, dp):
-        pl.semaphore_signal(
-            barrier, inc=1, device_id={"dp": z_peer(r)}, device_id_type=MESH
-        )
+    for peer in greeted:
+        pl.semaphore_signal(barrier, inc=1, device_id={"dp": peer}, device_id_type=MESH)
     for x in range(n - 1, 0, -1):
         pl.semaphore_signal(
             barrier, inc=1, device_id={"fsdp": relative(x)}, device_id_type=MESH
@@ -455,7 +457,9 @@
         meta = jnp.where((sub == 0) & here, rows_s[j], meta)
         meta = jnp.where((sub == 1) & here, cols_s[j], meta)
     meta_v[0] = meta
-    pl.semaphore_wait(barrier, n - 1 + dp - 1)
+    pl.semaphore_wait(barrier, n - 1 + len(greeted))
+    if dp == 4:
+        pl.semaphore_signal(ready, inc=1, device_id={"dp": z_near}, device_id_type=MESH)
 
     for x in range(n - 1, 0, -1):
         pltpu.make_async_remote_copy(
@@ -625,8 +629,6 @@
         )
 
     handed = half // 2 if dp == 4 else 0
-    z_near = z + 1 - 2 * lax.rem(z, 2)
-    z_far = z + 2 - 4 * lax.rem(z // 2, 2)
 
     def z_sum(c, squares):
         piece = fin[c, z_rows(z)]
@@ -650,11 +652,6 @@
     def a_hand(c):
         a_copy(c, z, z_far, zf_rs.at[c]).wait_recv()
         a_copy(c, z_far, z_near, zb_rs).start()
-
-    def z_cross(c, squares):
-        squares = z_sum(c, squares)
-        a_cross(c)
-        return squares
 
     def z_step(c, squares):
         squares = z_sum(c, squares)
@@ -697,15 +694,17 @@
     full = collect(far, known)
     full_v[1] = full
     to_smem(1).start()
+    for e in sent[1:]:
+        foreign(e, full)
     own(sent[0])
     to_smem(1).wait()
-    for k in range(1, len(sent)):
-        foreign(sent[k])
-        pass_on(sent[k - 1], [0])
-        own(sent[k])
+    pass_on(sent[0], [0, 1])
+    for e in sent[1:]:
+        own(e)
     foreign(kept[0])
-    pass_on(sent[-1], [0])
-    for c in range(1, half - 1):
+    for e in sent[1:]:
+        pass_on(e, [0, 1])
+    for c in range(2, half - 1):
         for e in sent:
             pass_on(e, [c])
     for e in kept[1:]:
@@ -762,6 +761,8 @@
         return carry
 
     lax.fori_loop(1, half - 1, second, 0)
+    if dp == 4:
+        pl.semaphore_wait(ready, 1)
     for t in range(2, stages):
         reduce_step(t, 0)
     reduce_step(1, half - 1)
@@ -782,7 +783,9 @@
                     ag_wait(i - 1, e - 2 ** (i - 1), h)
                     ag_send(p, i, e, h)
 
-    squares = lax.fori_loop(0, handed, z_cross, jnp.zeros((8, 128), F32))
+    squares = lax.fori_loop(0, handed, z_sum, jnp.zeros((8, 128), F32))
+    for c in range(handed):
+        a_cross(c)
     squares = lax.fori_loop(handed, half // 2, z_step, squares)
     for i in range(1, chip_bits):
         ag_pass(i, 0, 1)
@@ -804,9 +807,9 @@
             for h in range(2):
                 ag_pass(i, e, h)
     crossed = [x for x in near if x > 1 and x % 2 == 1]
+    project_all(crossed)
     for c in range(handed):
         a_hand(c)
-    project_all(crossed)
     project_all(far)
 
     entries = full_s[1, 2, 0]
@@ -905,6 +908,7 @@
             dma((8,)), dma((6,)), dma((2,)),
             dma((n - 1 + max(stages - 2, 0),)),
             dma((n // 2,)), dma((stages - 1, half)), dma((half,)), dma, dma, dma((half,)), dma,
+            pltpu.SemaphoreType.REGULAR,
         ],
         compiler_params=pltpu.CompilerParams(
             collective_id=0, has_side_effects=True, vmem_limit_bytes=44 * 2 ** 20

time: 38.2 us -> 37.2 us (0.974)
  Pallas kernels: 36.7 us -> 35.7 us
    pallas_call x1, Pallas kernels: 33 us -> 32 us  [fused(): pl.pallas_call(functools.partial(fused_kernel, n, dp, root), out_shape=(p...]
where the time goes in v7:
time: 37.2 us; the launch traced here: 37 us
  Pallas kernels  35.7 us (96%)
  between operations  1.29 us (3%)
    pallas_call x1, Pallas kernels, fused(): pl.pallas_call(functools.partial(fused_kernel, n, dp, root), out_shape=(p...  32 us
    pallas_call x1, Pallas kernels, fused(): pl.pallas_call(write_kernel, out_shape=(jax.ShapeDtypeStruct(cotangent.sh...  3.73 us

profile of v7, /device:TPU:0, one launch (start us, length us, event | category | flops | bytes accessed | tf_op | source)
XLA Modules:
  0.0 37.0 jit_solution(7854358081872282864)
XLA Ops:
  1.3 32.0 %fused.1 = (bf16[65,256,128]{2,1,0:T(8,128)(2,1)S(1)}, bf16[65,256,128]{2,1,0:T(8,128)(2,1)S(1)}, f32[8,128,128]{2,1,0:T(8,128)S(1)}, s32[8,128]{1,0:T(8,128)S(4)}) custom-call(s32[8]{0:T(128)} %rows_hbm.1, s32[8]{0:T(128)} %cols_hbm.1, s32[1]{0:T(128)S(6)} %copy.9.cnt_s, bf16[8,128,128]{2,1,0:T(8,128)(2,1)} %tiles_hbm.1, bf16[256,14336]{1,0:T(8,128)(2,1)} %hid_hbm.1, ...), custom_call_target="tpu_custom_call" | custom-call | tf_op jit(solution)/shard_map/fused/pallas_call | solution.py:878
  33.3 3.7 %write.1 = (bf16[256,4096]{1,0:T(8,128)(2,1)}, bf16[256,14336]{1,0:T(8,128)(2,1)}, f32[8,128,128]{2,1,0:T(8,128)}) custom-call(bf16[65,256,128]{2,1,0:T(8,128)(2,1)S(1)} %get-tuple-element.7.grad_v, bf16[65,256,128]{2,1,0:T(8,128)(2,1)S(1)} %get-tuple-element.8.layer_v, f32[8,128,128]{2,1,0:T(8,128)S(1)} %get-tuple-element.9.wg_v, ...), custom_call_target="tpu_custom_call" | custom-call | tf_op jit(solution)/shard_map/write/pallas_call | solution.py:918

commit v8 on v7

--- a/solution.py
+++ b/solution.py
@@ -461,7 +461,7 @@
     if dp == 4:
         pl.semaphore_signal(ready, inc=1, device_id={"dp": z_near}, device_id_type=MESH)
 
-    for x in range(n - 1, 0, -1):
+    for x in near[:0:-1] + far:
         pltpu.make_async_remote_copy(
             meta_v.at[0], meta_v.at[place[x]], send_sem.at[0], meta_rs.at[int(x in far)],
             device_id={"fsdp": relative(x)}, device_id_type=MESH,

time: 37.2 us -> 37 us (level)
  no operation moved by 1% of the time
where the time goes in v8:
time: 37 us; the launch traced here: 36.9 us
  Pallas kernels  35.6 us (96%)
  between operations  1.29 us (3%)
    pallas_call x1, Pallas kernels, fused(): pl.pallas_call(functools.partial(fused_kernel, n, dp, root), out_shape=(p...  31.9 us
    pallas_call x1, Pallas kernels, fused(): pl.pallas_call(write_kernel, out_shape=(jax.ShapeDtypeStruct(cotangent.sh...  3.73 us

profile of v8, /device:TPU:0, one launch (start us, length us, event | category | flops | bytes accessed | tf_op | source)
XLA Modules:
  0.0 36.9 jit_solution(1292516414308423404)
XLA Ops:
  1.3 31.9 %fused.1 = (bf16[65,256,128]{2,1,0:T(8,128)(2,1)S(1)}, bf16[65,256,128]{2,1,0:T(8,128)(2,1)S(1)}, f32[8,128,128]{2,1,0:T(8,128)S(1)}, s32[8,128]{1,0:T(8,128)S(4)}) custom-call(s32[8]{0:T(128)} %rows_hbm.1, s32[8]{0:T(128)} %cols_hbm.1, s32[1]{0:T(128)S(6)} %copy.9.cnt_s, bf16[8,128,128]{2,1,0:T(8,128)(2,1)} %tiles_hbm.1, bf16[256,14336]{1,0:T(8,128)(2,1)} %hid_hbm.1, ...), custom_call_target="tpu_custom_call" | custom-call | tf_op jit(solution)/shard_map/fused/pallas_call | solution.py:878
  33.1 3.7 %write.1 = (bf16[256,4096]{1,0:T(8,128)(2,1)}, bf16[256,14336]{1,0:T(8,128)(2,1)}, f32[8,128,128]{2,1,0:T(8,128)}) custom-call(bf16[65,256,128]{2,1,0:T(8,128)(2,1)S(1)} %get-tuple-element.7.grad_v, bf16[65,256,128]{2,1,0:T(8,128)(2,1)S(1)} %get-tuple-element.8.layer_v, f32[8,128,128]{2,1,0:T(8,128)S(1)} %get-tuple-element.9.wg_v, ...), custom_call_target="tpu_custom_call" | custom-call | tf_op jit(solution)/shard_map/write/pallas_call | solution.py:918
